TPU v7x, 32 devices: a whole 2x2x4 slice. The times are simulated.
32 devices in a mesh: task: 2 (over core), row: 16 (over z, y, x).
Axes of the slice: x: 2, y: 2, z: 4, core: 2. Of those that a mesh axis runs over, the one named last changes fastest.
Arguments:
- activation_grams: float32 [2, 7168, 7168], P('task', 'row'), may hold values from -240 to 240, as said below
- adjusted_weights: bfloat16 [2, 7168, 2048], P('task', 'row'), may hold values from -0.59765625 to 0.59765625
Outputs:
- reduced_gram: float32 [7168, 7168], P('row')
- reduced_rhs: float32 [7168, 2048], P('row')
Inputs may be any that keep to these rules, and one draw needn't show every extreme that they name: Each activation_grams[m] is symmetric and positive definite.
All inputs are finite; a program needn't handle non-finite values.
Results may differ from a plain program's by a relative error of at most 0.0003.
Values may be sent and summed in bfloat16 or wider, within the bound.
No kernel may reach another device: no remote copies, remote signals or barrier semaphores. Data moves between devices by JAX's collectives and lax.ppermute only.
A program may use at most 192 MiB of HBM per device.

v0:
```python
import jax
import jax.numpy as jnp
from jax import lax
from jax.sharding import PartitionSpec as P

PANEL_STEPS = 2


def broadcast(value, axis, source):
    kept = jnp.where(lax.axis_index(axis) == source, value, 0).astype(value.dtype)
    return lax.psum(kept, axis)


def product(left, right):
    return jnp.dot(left, right, precision=lax.Precision.HIGHEST)


def per_device(activation_grams, adjusted_weights):
    local_models, rows, width = activation_grams.shape
    columns = adjusted_weights.shape[2]
    position = lax.axis_index("row")
    start_col = position * rows
    own_block = lax.dynamic_slice_in_dim(activation_grams, start_col, rows, 2)
    diagonal_entries = jnp.diagonal(own_block, axis1=1, axis2=2)
    total_trace = lax.psum(jnp.sum(diagonal_entries, axis=1), "row")
    scaling = width / total_trace
    identity_block = jnp.eye(rows, dtype=jnp.float32)
    new_block = 0.9 * own_block + 0.1 * (diagonal_entries[:, :, None] * identity_block)
    regular = lax.dynamic_update_slice_in_dim(0.9 * activation_grams, new_block, start_col, 2)
    source = scaling[:, None, None] * regular
    form = "mbn,mnd->bd"
    initial = jnp.zeros((rows, columns), jnp.float32)
    piece = lax.all_gather(adjusted_weights, "row", axis=1, tiled=True)
    chosen = lax.slice_in_dim(source, 0, piece.shape[1], axis=2)
    folded = initial + jnp.einsum(
        form, chosen, piece.astype(jnp.float32), precision=lax.Precision.HIGHEST
    )
    merged_part = jnp.sum(source, axis=0)
    merged_rows, rhs_rows = lax.psum((merged_part, folded), "task")
    for panel in range(PANEL_STEPS):
        diag_block = lax.dynamic_slice_in_dim(merged_rows, start_col, rows, 1)
        diag_block = jnp.where(position >= panel, diag_block, identity_block)
        factor = jnp.linalg.cholesky(diag_block)
        upper_rows = jax.scipy.linalg.solve_triangular(factor, merged_rows, lower=True)
        solved_rows = jax.scipy.linalg.solve_triangular(factor, rhs_rows, lower=True)
        upper_rows, solved_rows = (
            broadcast(upper_rows, "row", panel),
            broadcast(solved_rows, "row", panel),
        )
        mine = lax.dynamic_slice_in_dim(upper_rows, start_col, rows, 1).T
        merged_next = merged_rows - product(mine, upper_rows)
        rhs_next = rhs_rows - product(mine, solved_rows)
        merged_rows = jnp.where(
            position == panel, upper_rows, jnp.where(position > panel, merged_next, merged_rows)
        )
        rhs_rows = jnp.where(
            position == panel, solved_rows, jnp.where(position > panel, rhs_next, rhs_rows)
        )
    return (merged_rows, rhs_rows)


def solution(mesh):
    placed = (P("task", "row", None), P("task", "row", None))
    return jax.shard_map(
        per_device,
        mesh=mesh,
        in_specs=placed,
        out_specs=(P("row", None), P("row", None)),
        check_vma=False,
    )
```

profile of v0, /device:TPU:0, one launch (start us, length us, event | category | flops | bytes accessed | tf_op | source)
XLA Modules:
  0.0 1975.7 jit_solution(9161190287944961805)
XLA Ops:
  7.9 14.6 copy.34
  23.9 3.9 gather_fusion
  28.5 45.8 %psum.49 = f32[1]{0:T(128)} all-reduce(f32[1]{0:T(128)} %bitcast.2), channel_id=1, replica_groups=mesh['task'=2,'row'=16] {'row'}, use_global_device_ids=true, to_apply=%region_1.2 | all-reduce | flops 1 | bytes 8 | tf_op jit(solution)/shard_map/psum | solution.py:25
  75.0 12.2 broadcast_multiply_fusion
  87.1 2.3 add_dynamic-update-slice_fusion
  89.4 12.3 multiply_bitcast_fusion
  101.7 222.6 %all-gather.2.cloned.1.call-done = bf16[1,7168,2048]{2,1,0:T(8,128)(2,1)} async-done(((bf16[1,448,2048]{2,1,0:T(8,128)(2,1)}), bf16[1,7168,2048]{2,1,0:T(8,128)(2,1)}) %all-gather.2.cloned.1.call-update) | async-done | bytes 29360144 | tf_op jit(solution)/shard_map/all_gather | solution.py:33
  324.3 47.4 %fusion = f32[448,2048]{1,0:T(8,128)} fusion(f32[448,7168]{0,1:T(8,128)} %multiply_bitcast_fusion, bf16[1,7168,2048]{2,1,0:T(8,128)(2,1)} %all-gather.2.cloned.1.call-done), kind=kOutput, calls=%fused_computation.5 | convolution fusion | flops 78920024064 | bytes 45875200 | tf_op jit(solution)/shard_map/mbn,mnd->bd/dot_general | solution.py:35
  372.0 61.9 %all-reduce.16.cloned.1.call-done = (f32[448,7168]{0,1:T(8,128)}, f32[448,2048]{1,0:T(8,128)}) async-done(((f32[448,7168]{0,1:T(8,128)}, f32[448,2048]{1,0:T(8,128)}), (f32[448,7168]{0,1:T(8,128)}, f32[448,2048]{1,0:T(8,128)})) %all-reduce.16.cloned.1.call-update) | async-done | bytes 16515088 | tf_op jit(solution)/shard_map/psum | solution.py:39
  437.0 11.7 cholesky.292
  448.8 9.8 custom-call.33
  459.3 11.7 cholesky.311
  471.0 10.2 custom-call.34
  481.8 11.7 cholesky.332
  494.2 9.8 custom-call.35
  505.3 5.8 cholesky.352
  516.1 9.0 while.8
  516.8 2.3 bitcast_dynamic-update-slice_fusion.4
  519.7 2.3 bitcast_dynamic-update-slice_fusion.4
  522.7 2.3 bitcast_dynamic-update-slice_fusion.4
  525.2 39.5 %custom-call.36 = f32[4,128,128]{1,2,0:T(8,128)S(1)} custom-call(f32[4,128,128]{2,1,0:T(8,128)S(1)} %pad_maximum_fusion), custom_call_target="InvertDiagBlocksLowerTriangular" | custom-call | tf_op jit(solution)/shard_map/jit(_solve_triangular)/triangular_solve | solution.py:44
  564.7 5.7 fusion.32
  570.5 9.4 convolution_subtract_fusion.3
  579.9 3.8 fusion.105
  583.7 12.8 convolution_subtract_fusion.2
  596.6 5.2 fusion.107
  601.7 21.1 %fusion.19 = f32[64,7168]{0,1:T(8,128)} fusion(f32[128,7168]{1,0:T(8,128)} %fusion.107, f32[128,7168]{1,0:T(8,128)} %copy-done.3, f32[128,7168]{1,0:T(8,128)S(1)} %fusion.32, f32[448,7168]{0,1:T(8,128)S(1)} %bitcast.150, f32[448,448]{1,0:T(8,128)S(1)} %copy-done.18), kind=kOutput, calls=%fused_computation.31 | convolution fusion | flops 2119892992 | bytes 16613376 | tf_op jit(solution)/shard_map/jit(_solve_triangular)/triangular_solve | solution.py:44
  622.9 5.3 copy.43
  628.1 5.2 copy.42
  633.4 5.4 copy.41
  638.8 2.3 fusion.60
  641.0 2.2 convolution_subtract_fusion.7
  644.3 2.5 convolution_subtract_fusion.5
  647.9 3.1 fusion.49
  651.6 3.5 fusion.119
  659.6 5.7 maximum_select_fusion
  665.4 488.1 %all-reduce.14.cloned.1.call-done = (f32[448,7168]{0,1:T(8,128)}, f32[448,2048]{1,0:T(8,128)}) async-done(((f32[448,7168]{0,1:T(8,128)}, f32[448,2048]{1,0:T(8,128)}), (f32[448,7168]{0,1:T(8,128)}, f32[448,2048]{1,0:T(8,128)})) %all-reduce.14.cloned.1.call-update) | async-done | bytes 16515088 | tf_op jit(solution)/shard_map/psum | solution.py:11
  1153.5 33.6 %fusion.2 = f32[448,7168]{0,1:T(8,128)S(1)} fusion(f32[448,7168]{0,1:T(8,128)} %get-tuple-element.61, f32[448,7168]{0,1:T(8,128)} %get-tuple-element.63, pred[]{:T(512)S(6)} %gt.8, pred[]{:T(512)S(6)} %eq.27, s32[]{:T(128)S(6)} %select_n.105), kind=kOutput, calls=%fused_computation.9 | convolution fusion | flops 17273389056 | bytes 57802760 | tf_op jit(solution)/shard_map/dot_general | solution.py:15
  1187.1 5.2 copy-done
  1194.1 11.7 cholesky.368
  1206.0 9.8 custom-call.37
  1216.4 11.7 cholesky.387
  1229.5 10.0 custom-call.38
  1240.0 11.7 cholesky.408
  1252.5 9.8 custom-call.39
  1263.5 5.8 cholesky.428
  1273.6 8.5 while.9
  1282.2 39.5 %custom-call.40 = f32[4,128,128]{1,2,0:T(8,128)S(1)} custom-call(f32[4,128,128]{2,1,0:T(8,128)S(1)} %pad_maximum_fusion.1), custom_call_target="InvertDiagBlocksLowerTriangular" | custom-call | tf_op jit(solution)/shard_map/jit(_solve_triangular)/triangular_solve | solution.py:44
  1321.8 5.7 fusion.30
  1327.6 9.4 convolution_subtract_fusion.1
  1337.0 4.1 fusion.109
  1341.1 12.5 convolution_subtract_fusion
  1353.6 5.2 fusion.111
  1358.8 21.1 %fusion.16 = f32[64,7168]{0,1:T(8,128)} fusion(f32[128,7168]{1,0:T(8,128)} %fusion.111, f32[128,7168]{1,0:T(8,128)} %copy-done.4, f32[128,7168]{1,0:T(8,128)S(1)} %fusion.30, f32[448,7168]{0,1:T(8,128)S(1)} %bitcast.148, f32[448,448]{1,0:T(8,128)S(1)} %copy-done.16), kind=kOutput, calls=%fused_computation.30 | convolution fusion | flops 2119892992 | bytes 16613376 | tf_op jit(solution)/shard_map/jit(_solve_triangular)/triangular_solve | solution.py:44
  1379.9 5.3 copy.52
  1385.2 5.2 copy.51
  1390.4 5.2 copy.50
  1395.7 10.0 fusion.28
  1413.8 3.5 fusion.121
  1421.7 5.7 maximum_select_fusion.1
  1427.5 483.9 %all-reduce.12.cloned.1.call-done = (f32[448,7168]{0,1:T(8,128)}, f32[448,2048]{1,0:T(8,128)}) async-done(((f32[448,7168]{0,1:T(8,128)}, f32[448,2048]{1,0:T(8,128)}), (f32[448,7168]{0,1:T(8,128)}, f32[448,2048]{1,0:T(8,128)})) %all-reduce.12.cloned.1.call-update) | async-done | bytes 16515088 | tf_op jit(solution)/shard_map/psum | solution.py:11
  1911.4 33.6 %fusion.3 = f32[448,7168]{0,1:T(8,128)} fusion(f32[448,7168]{0,1:T(8,128)} %get-tuple-element.59, f32[448,7168]{0,1:T(8,128)} %copy-done, pred[]{:T(512)S(6)} %gt.9, pred[]{:T(512)S(6)} %eq.26, s32[]{:T(128)S(6)} %select_n.105), kind=kOutput, calls=%fused_computation.10 | convolution fusion | flops 17273389056 | bytes 57802760 | tf_op jit(solution)/shard_map/dot_general | solution.py:15
  1945.1 9.1 fusion.29
  1954.2 14.6 copy.55
  (154 shorter events, 50.2 us)
Async XLA Ops:
  7.2 317.2 %all-gather.2.cloned.1.call-start = ((), (), s32[]{:S(2)}) async-start(), calls=%async_computation | async-start | bytes 31195136 | tf_op jit(solution)/shard_map/all_gather | solution.py:33
  7.9 426.0 %all-reduce.16.cloned.1.call-start = ((), (), s32[]{:S(2)}) async-start(), calls=%async_computation.3 | async-start | bytes 36700160 | tf_op jit(solution)/shard_map/psum | solution.py:39
  371.7 781.8 %all-reduce.14.cloned.1.call-start = ((), (), s32[]{:S(2)}) async-start(), calls=%async_computation.2 | async-start | bytes 36700160 | tf_op jit(solution)/shard_map/psum | solution.py:11
  436.9 44.8 %copy-start.21 = (f32[448,448]{1,0:T(8,128)}, f32[448,448]{1,0:T(8,128)S(1)}, u32[]{:S(2)}) copy-start(f32[448,448]{1,0:T(8,128)S(1)} %fusion.63) | copy-start | bytes 2408452
  493.5 90.2 %slice-start.4 = ((s8[14680064]{0:T(1024)(128)(4,1)}), s8[2097152]{0:T(1024)(128)(4,1)S(1)}, s32[]{:S(2)}) async-start(s8[14680064]{0:T(1024)(128)(4,1)} %bitcast.149), calls=%async_computation.8 | async-start | bytes 4194304
  515.2 0.9 copy-start.17
  564.7 5.8 copy-start.18
  564.7 19.0 slice-start.5
  570.4 31.3 %copy-start.1 = (f32[128,7168]{1,0:T(8,128)}, f32[128,7168]{1,0:T(8,128)S(1)}, u32[]{:S(2)}) copy-start(f32[128,7168]{1,0:T(8,128)S(1)} %fusion.32) | copy-start | bytes 11010052
  570.5 13.3 slice-start.6
  570.5 13.3 slice-start.7
  583.7 12.8 copy-start.3
  646.8 4.8 copy-start.14
  651.6 5.6 copy-start.13
  655.1 3.4 copy-start.10
  655.1 4.5 copy-start.12
  665.4 1246.1 %all-reduce.12.cloned.1.call-start = ((), (), s32[]{:S(2)}) async-start(), calls=%async_computation.1 | async-start | bytes 36700160 | tf_op jit(solution)/shard_map/psum | solution.py:11
  1187.1 5.2 copy-start
  1194.1 57.6 %copy-start.20 = (f32[448,448]{1,0:T(8,128)}, f32[448,448]{1,0:T(8,128)S(1)}, u32[]{:S(2)}) copy-start(f32[448,448]{1,0:T(8,128)S(1)} %fusion.62) | copy-start | bytes 2408452
  1251.8 89.3 %slice-start = ((s8[14680064]{0:T(1024)(128)(4,1)}), s8[2097152]{0:T(1024)(128)(4,1)S(1)}, s32[]{:S(2)}) async-start(s8[14680064]{0:T(1024)(128)(4,1)} %bitcast.147), calls=%async_computation.4 | async-start | bytes 4194304
  1272.7 0.9 copy-start.15
  1321.8 5.8 copy-start.16
  1321.8 19.3 slice-start.1
  1327.5 31.2 %copy-start.2 = (f32[128,7168]{1,0:T(8,128)}, f32[128,7168]{1,0:T(8,128)S(1)}, u32[]{:S(2)}) copy-start(f32[128,7168]{1,0:T(8,128)S(1)} %fusion.30) | copy-start | bytes 11010052
  1327.6 13.5 slice-start.2
  1327.6 13.5 slice-start.3
  1341.1 12.5 copy-start.4
  1405.7 5.5 copy-start.5
  1410.0 3.7 copy-start.11
  1413.8 5.6 copy-start.9
  1417.2 3.4 copy-start.7
  1417.2 4.5 copy-start.8
  1911.4 33.6 %copy-start.6 = (f32[448,2048]{1,0:T(8,128)S(1)}, f32[448,2048]{1,0:T(8,128)}, u32[]{:S(2)}) copy-start(f32[448,2048]{1,0:T(8,128)} %copy-done.5) | copy-start | bytes 11010052
  1911.4 33.6 %copy-start.19 = (f32[448,2048]{1,0:T(8,128)S(1)}, f32[448,2048]{1,0:T(8,128)}, u32[]{:S(2)}) copy-start(f32[448,2048]{1,0:T(8,128)} %get-tuple-element.60) | copy-start | bytes 11010052
Sparse Core Ops, SparseCore 0:
  10.7 313.5 all-gather.1
  371.9 62.0 all-reduce.15
  665.5 487.9 all-reduce.13
  1427.6 483.7 all-reduce.11
where the time goes:
time: 1980 us
  waiting for transfers between devices  1260 us (64%)
  matrix products  282 us (14%)
  other arithmetic  273 us (14%)
  local copies, waits for them, and re-layouts  96.1 us (5%)
  blocking collectives  45.8 us (2%)
  between operations  21.1 us (1%)
    psum x2, waiting for transfers between devices, broadcast(): return lax.psum(kept, axis)  972 us
    all_gather x1, waiting for transfers between devices, per_device(): piece = lax.all_gather(adjusted_weights, 'row', axis=1, tiled=True)  223 us
    another operation x29, other arithmetic, per_device(): factor = jnp.linalg.cholesky(diag_block)  146 us
    another operation x14, matrix products, per_device(): jax.scipy.linalg.solve_triangular(factor, merged_rows, lower=True)  123 us
    dot_general x4, matrix products, product(): return jnp.dot(left, right, precision=lax.Precision.HIGHEST)  86.3 us
    another operation x11, other arithmetic, per_device(): jax.scipy.linalg.solve_triangular(factor, merged_rows, lower=True)  79.5 us
    psum x1, waiting for transfers between devices, per_device(): merged_rows, rhs_rows = lax.psum((merged_part, folded), 'task')  61.9 us
    another operation x29, local copies, waits for them, and re-layouts, per_device(): jax.scipy.linalg.solve_triangular(factor, merged_rows, lower=True)  49 us
  transfers between devices with their start and end apart: 4, of which 4 were waited for; matrix products, arithmetic and copies ran while one was open for 2% of the time, Pallas kernels for 0%

commit v1 on v0

v1 whole, which is shorter than its diff:
```python
import functools
import itertools
import math

import jax
import jax.numpy as jnp
from jax import lax
from jax.experimental import pallas as pl
from jax.experimental.pallas import tpu as pltpu
from jax.sharding import PartitionSpec as P


PANEL_STEPS = 2
BLOCK = 128
GROUP = 8
EXACT = lax.Precision.HIGHEST
THREE = lax.Precision.HIGH


def dot(a, b, dims, precision):
    return lax.dot_general(
        a, b, (dims, ((), ())), precision=precision, preferred_element_type=jnp.float32
    )


def invert_block(d_ref, x_ref):
    row = lax.broadcasted_iota(jnp.int32, (BLOCK, BLOCK), 0)
    lane = lax.broadcasted_iota(jnp.int32, (BLOCK, BLOCK), 1)
    x_ref[...] = jnp.where(row == lane, 1.0, 0.0).astype(jnp.float32)
    lanes = lax.broadcasted_iota(jnp.int32, (GROUP, BLOCK), 1)

    def body(step, carry):
        top = d_ref[0:GROUP, :]
        mirror = x_ref[0:GROUP, :]
        small = {}
        for i in range(GROUP):
            for k in range(i, GROUP):
                small[i, k] = jnp.broadcast_to(top[i : i + 1, k : k + 1], (1, BLOCK))
        us = [top[i : i + 1, :] for i in range(GROUP)]
        xs = [mirror[i : i + 1, :] for i in range(GROUP)]
        for i in range(GROUP):
            pivot = small[i, i]
            root = lax.rsqrt(pivot)
            root = root * (1.5 - 0.5 * pivot * root * root)
            us[i] = us[i] * root
            xs[i] = xs[i] * root
            ratio = {k: small[i, k] * root for k in range(i + 1, GROUP)}
            for k in range(i + 1, GROUP):
                for j in range(k, GROUP):
                    small[k, j] = small[k, j] - ratio[k] * ratio[j]
                us[k] = us[k] - ratio[k] * us[i]
                xs[k] = xs[k] - ratio[k] * xs[i]
        u = jnp.concatenate(us, axis=0)
        x = jnp.concatenate(xs, axis=0)
        left = jnp.where(lanes < BLOCK - GROUP * step, u, 0.0)
        d_new = d_ref[GROUP:, :] - dot(left, u, ((0,), (0,)), EXACT)[GROUP:, :]
        x_new = x_ref[GROUP:, :] - dot(left, x, ((0,), (0,)), EXACT)[GROUP:, :]
        d_ref[0 : BLOCK - GROUP, :] = pltpu.roll(d_new, BLOCK - GROUP, 1)
        d_ref[BLOCK - GROUP :, :] = jnp.zeros((GROUP, BLOCK), jnp.float32)
        x_ref[0 : BLOCK - GROUP, :] = x_new
        x_ref[BLOCK - GROUP :, :] = x
        return carry

    lax.fori_loop(0, BLOCK // GROUP, body, 0)


def factor_body(blocks, a_ref, done_ref, w_ref, out_ref, d_ref, x_ref):
    n = a_ref.shape[0]
    w_ref[...] = a_ref[...]
    out_ref[...] = done_ref[...]
    for low in blocks:
        high = low + BLOCK
        d_ref[...] = w_ref[low:high, low:high]
        invert_block(d_ref, x_ref)
        x = x_ref[...]
        out_ref[low:high, low:high] = x
        if low:
            out_ref[low:high, :low] = dot(x, out_ref[low:high, :low], ((1,), (0,)), EXACT)
        if high < n:
            below = dot(w_ref[high:, low:high], x, ((1,), (1,)), EXACT)
            w_ref[high:, high:] = w_ref[high:, high:] - dot(below, below, ((1,), (1,)), EXACT)
            out_ref[high:, :high] = out_ref[high:, :high] - dot(
                below, out_ref[low:high, :high], ((1,), (0,)), EXACT
            )


def eliminate(blocks, a, done):
    n = a.shape[0]
    whole = jax.ShapeDtypeStruct((n, n), jnp.float32)
    return pl.pallas_call(
        functools.partial(factor_body, blocks),
        out_shape=(whole, whole),
        scratch_shapes=[
            pltpu.VMEM((BLOCK, BLOCK), jnp.float32),
            pltpu.VMEM((BLOCK, BLOCK), jnp.float32),
        ],
        cost_estimate=pl.CostEstimate(
            flops=20_000_000_000, bytes_accessed=16 * n * n, transcendentals=n
        ),
    )(a, done)


def inverse_factor(a):
    n = a.shape[0]
    full = -(-n // BLOCK) * BLOCK
    if full != n:
        index = jnp.arange(full)
        a = jnp.pad(a, ((0, full - n), (0, full - n)))
        a = jnp.where((index[:, None] == index[None, :]) & (index[:, None] >= n), 1.0, a)
    blocks = range(0, full, BLOCK)
    cut = len(blocks) // 2
    rest, done = eliminate(blocks[:cut], a, jnp.zeros((full, full), jnp.float32))
    done = eliminate(blocks[cut:], rest, done)[1]
    return done[:n, :n]


def torus_of(count):
    side = math.isqrt(count // 4) if count % 4 == 0 else 0
    return (4, side, side) if side and 4 * side * side == count else (count, 1, 1)


def shifted(value, torus, dim, by):
    pairs = []
    count = math.prod(torus)
    inner = math.prod(torus[dim + 1 :])
    size = torus[dim]
    for source in range(count):
        at = (source // inner) % size
        pairs.append((source, source + ((at + by) % size - at) * inner))
    return lax.ppermute(value, "row", pairs)


def blank(shape, dtype):
    return pl.pallas_call(
        lambda out_ref: None,
        out_shape=jax.ShapeDtypeStruct(shape, dtype),
        out_specs=pl.BlockSpec(memory_space=pl.ANY),
    )()


def along(torus, dim):
    return (lax.axis_index("row") // math.prod(torus[dim + 1 :])) % torus[dim]


def arrivals(value, torus, dim):
    size = torus[dim]
    at = along(torus, dim)
    items = []
    up = down = value
    for step in range(1, (size - 1) // 2 + 1):
        up = shifted(up, torus, dim, 1)
        down = shifted(down, torus, dim, -1)
        items += [(up, {dim: (at - step) % size}), (down, {dim: (at + step) % size})]
    if size == 2:
        items.append((shifted(value, torus, dim, 1), {dim: 1 - at}))
    elif size % 2 == 0:
        cut = next((d for d in range(3) if value.shape[d] % 2 == 0), 3)
        half = value.shape[cut] // 2
        far = (at + size // 2) % size
        first = shifted(lax.slice_in_dim(up, 0, half, axis=cut), torus, dim, 1)
        second = lax.slice_in_dim(down, half, value.shape[cut], axis=cut)
        second = shifted(second, torus, dim, -1)
        items += [(first, {dim: far}), (second, {dim: far, cut: half})]
    return items


def fill(buffer, items, lane=0):
    for chunk, at in items:
        start = [at.get(d, 0) for d in range(4)] + [lane]
        buffer = lax.dynamic_update_slice(
            buffer, chunk, tuple(jnp.asarray(i, jnp.int32) for i in start)
        )
    return buffer


def moved(items, by):
    return [(chunk, {**at, 0: at.get(0, 0) + by}) for chunk, at in items]


def gather_along(value, torus, dim):
    shape = list(value.shape)
    shape[dim] = torus[dim]
    buffer = fill(blank(tuple(shape), value.dtype), [(value, {dim: along(torus, dim)})])
    return fill(buffer, arrivals(value, torus, dim))


def widths_of(total):
    unit = 128 if total % 128 == 0 and total >= 512 else 1
    last = total // unit // 4 if total // unit >= 12 else total // unit // 7
    first = (total // unit - last) // 2
    return (first * unit, total - (first + last) * unit, last * unit)


def after(value, *others):
    return lax.optimization_barrier((value, *others))[0]


def torus_sum(value, torus, dims):
    total = value
    for shift in itertools.product(*(range(torus[d]) for d in dims)):
        if any(shift):
            pairs = []
            for source in range(math.prod(torus)):
                target = source
                for d, by in zip(dims, shift):
                    inner = math.prod(torus[d + 1 :])
                    at = (source // inner) % torus[d]
                    target += ((at + by) % torus[d] - at) * inner
                pairs.append((source, target))
            total = total + lax.ppermute(value, "row", pairs)
    return total


def spread(shard):
    return shard.reshape((1, 1, 1) + shard.shape)


def swapped(value):
    return lax.ppermute(value, "task", [(0, 1), (1, 0)])


def per_device(activation_grams, adjusted_weights):
    gram, weights = activation_grams[0], adjusted_weights[0]
    rows, width = gram.shape
    columns = weights.shape[1]
    panel = PANEL_STEPS * rows
    torus = torus_of(width // rows)
    position = lax.axis_index("row")
    start = position * rows

    def is_diagonal(shape, first):
        row = lax.broadcasted_iota(jnp.int32, shape, 0) + first
        return row == lax.broadcasted_iota(jnp.int32, shape, 1)

    def damped(block):
        return jnp.where(is_diagonal(block.shape, position * rows), block, 0.9 * block)

    reach = min(width, -(-rows // 128) * 128 + 128)
    first = jnp.minimum(start // 128 * 128, width - reach)
    near = lax.dynamic_slice_in_dim(gram, first, reach, 1)
    own_trace = jnp.sum(jnp.where(is_diagonal(near.shape, start - first), near, 0.0))
    trace = torus_sum(jnp.full((8, 128), own_trace), torus, (0,))

    own_panel = damped(gram[:, :panel])
    size0, size1, _ = widths_of(panel)
    split = size0 + size1
    late = gather_along(spread(own_panel[:, split:]), torus, 2)
    late = gather_along(late, torus, 1)
    early = gather_along(spread(own_panel[:, :split]), torus, 0)
    trace = torus_sum(trace, torus, (1, 2))
    scaling = width / trace[:1, :1]
    mid0 = gather_along(early[..., :size0], torus, 2)
    mid1 = gather_along(early[..., size0:], torus, 1)
    last = gather_along(late, torus, 0)
    ahead = arrivals(mid0[:1], torus, 1), arrivals(mid1[:1], torus, 2)
    behind = arrivals(mid0[1:], torus, 1), arrivals(mid1[1:], torus, 2)
    plane = blank((1,) + torus[1:] + (rows, panel), jnp.float32)
    panels = blank(torus + (rows, panel), jnp.float32)
    for lane, value, dim in ((0, mid0, 1), (size0, mid1, 2), (split, last, None)):
        at = {} if dim is None else {dim: along(torus, dim)}
        plane = fill(plane, [(value[:1], at)], lane)
        panels = fill(panels, [(value, at)], lane)
    plane = fill(plane, ahead[0], 0)
    plane = fill(plane, ahead[1], size0)
    panels = fill(panels, ahead[0], 0)
    panels = fill(panels, ahead[1], size0)
    panels = fill(panels, moved(behind[0], 1), 0)
    panels = fill(panels, moved(behind[1], 1), size0)
    panels = panels.reshape(width, panel)

    width0, width1, _ = widths_of(columns)
    fork = width0 + width1
    w_late = gather_along(spread(weights[:, fork:]), torus, 2)
    weights = after(weights, early[:1, :1, :1, :8, :128])
    w_early = gather_along(spread(weights[:, :fork]), torus, 0)
    w_late = gather_along(w_late, torus, 1)
    half0, half1 = width0 // 2, width1 // 2
    w_mids = []
    for turn, (size, dim) in enumerate(((half0, 2), (half1, 1), (width0 - half0, 2), (width1 - half1, 1))):
        first = (0, width0, half0, width0 + half1)[turn]
        w_mids.append(gather_along(w_early[..., first : first + size], torus, dim))
    gathered_weights = [gather_along(w_late, torus, 0)] + [
        gather_along(mid, torus, 1 if turn % 2 == 0 else 2)
        for turn, mid in enumerate(w_mids)
    ]
    gathered_weights = [w.reshape(width, -1) for w in gathered_weights]

    corner = scaling * plane.reshape(-1, panel)[:panel]
    corner = corner + swapped(corner)
    own = scaling * own_panel
    own = own + swapped(own)
    inverse = inverse_factor(corner)
    factored = position < PANEL_STEPS
    lead = lax.dynamic_slice_in_dim(inverse, jnp.minimum(position, PANEL_STEPS - 1) * rows, rows, 0)
    folded = dot(dot(own, inverse, ((1,), (1,)), EXACT), inverse, ((1,), (0,)), EXACT)
    transform = scaling * jnp.where(factored, lead, -folded)
    kept = jnp.where(factored, 0.0, scaling)
    reduced = kept * damped(gram) + dot(transform, panels, ((1,), (1,)), THREE)
    partner = swapped(reduced)
    reduced_gram = reduced + partner

    high = lax.reduce_precision(reduced, 8, 7)
    rest = (reduced - high).astype(jnp.bfloat16)
    both = jnp.concatenate([high.astype(jnp.bfloat16), rest], axis=0)
    solved = []
    for weight in gathered_weights:
        part = jnp.dot(both, weight, preferred_element_type=jnp.float32)
        part = part[:rows] + part[rows:]
        solved.append(part + swapped(part))
    return (reduced_gram, jnp.concatenate([solved[i] for i in (1, 3, 2, 4, 0)], axis=1))


def solution(mesh):
    placed = (P("task", "row", None), P("task", "row", None))
    return jax.shard_map(
        per_device,
        mesh=mesh,
        in_specs=placed,
        out_specs=(P("row", None), P("row", None)),
        check_vma=False,
    )
```

time: 1980 us -> 979 us (0.49)
  waiting for transfers between devices: 1260 us -> 546 us
  other arithmetic: 273 us -> 30.7 us
  matrix products: 282 us -> 93.7 us
  Pallas kernels: 0 us -> 88.5 us
  starting transfers between devices: 0.37 us -> 77.7 us
  blocking collectives: 45.8 us -> 0 us
  local copies, waits for them, and re-layouts: 96.1 us -> 132 us
    psum x3 -> x0, waiting for transfers between devices: 1030 us -> none  [the longest x2 972 us: broadcast(): return lax.psum(kept, axis)]
    ppermute x0 -> x48, waiting for transfers between devices: none -> 546 us  [the longest x34 537 us: shifted(): return lax.ppermute(value, 'row', pairs)]
    another operation x40 -> x0, other arithmetic: 226 us -> none  [the longest x29 146 us: per_device(): factor = jnp.linalg.cholesky(diag_block)]
    all_gather x1 -> x0, waiting for transfers between devices: 223 us -> none  [per_device(): piece = lax.all_gather(adjusted_weights, 'row', axis=1, tiled=True)]
    another operation x40 -> x0, matrix products: 148 us -> none  [the longest x14 123 us: per_device(): jax.scipy.linalg.solve_triangular(factor, merged_rows, lower=True)]
    dynamic_update_slice x0 -> x52, local copies, waits for them, and re-layouts: none -> 95.4 us  [fill(): lax.dynamic_update_slice(buffer, chunk, tuple((jnp.asarray(i, jnp.int32)...]
    pallas_call x0 -> x22, Pallas kernels: none -> 88.5 us  [the longest x2 88.5 us: eliminate(): pl.pallas_call(functools.partial(factor_body, blocks), out_shape=(whole,...]
    ppermute x0 -> x48, starting transfers between devices: none -> 77.7 us  [the longest x34 65.2 us: shifted(): return lax.ppermute(value, 'row', pairs)]
  transfers between devices with their start and end apart: 4 -> 48, of which waited for: 4 -> 32; matrix products, arithmetic and copies ran while one was open for 2% -> 17% of each run, Pallas kernels for 0% -> 9%
where the time goes in v1:
time: 979 us; the launch traced here: 971 us
  waiting for transfers between devices  546 us (56%)
  local copies, waits for them, and re-layouts  132 us (13%)
  matrix products  93.7 us (10%)
  Pallas kernels  88.5 us (9%)
  starting transfers between devices  77.7 us (8%)
  other arithmetic  30.7 us (3%)
    ppermute x34, waiting for transfers between devices, shifted(): return lax.ppermute(value, 'row', pairs)  537 us
    dynamic_update_slice x52, local copies, waits for them, and re-layouts, fill(): lax.dynamic_update_slice(buffer, chunk, tuple((jnp.asarray(i, jnp.int32)...  95.4 us
    pallas_call x2, Pallas kernels, eliminate(): pl.pallas_call(functools.partial(factor_body, blocks), out_shape=(whole,...  88.5 us
    ppermute x34, starting transfers between devices, shifted(): return lax.ppermute(value, 'row', pairs)  65.2 us
    dot_general x5, matrix products, per_device(): part = jnp.dot(both, weight, preferred_element_type=jnp.float32)  51.6 us
    dot_general x3, matrix products, dot(): lax.dot_general(a, b, (dims, ((), ())), precision=precision, preferred_el...  42.1 us
  transfers between devices with their start and end apart: 48, of which 32 were waited for; matrix products, arithmetic and copies ran while one was open for 17% of the time, Pallas kernels for 9%

profile of v1, /device:TPU:0, one launch (start us, length us, event | category | flops | bytes accessed | tf_op | source)
XLA Modules:
  0.0 971.0 jit_solution(13981043720594957694)
XLA Ops:
  0.7 2.4 fusion.9
  3.8 3.1 collective-permute-start
  6.9 2.6 collective-permute-start.1
  18.9 2.3 collective-permute-done.5
  22.4 2.9 broadcast_multiply_fusion
  26.8 3.5 collective-permute-start.7
  30.4 31.2 %collective-permute-done.6 = f32[1,1,1,448,768]{4,3,2,1,0:T(8,128)S(1)} collective-permute-done((f32[1,1,1,448,768]{4,3,2,1,0:T(8,128)}, f32[1,1,1,448,768]{4,3,2,1,0:T(8,128)S(1)}, u32[]{:S(2)}, u32[]{:S(2)}) %collective-permute-start.6) | collective-permute-done | bytes 1376288 | tf_op jit(solution)/shard_map/ppermute | solution.py:130
  62.5 21.8 %collective-permute-start.8 = (f32[1,1,1,224,768]{4,3,2,1,0:T(8,128)}, f32[1,1,1,224,768]{4,3,2,1,0:T(8,128)}, u32[]{:S(2)}, u32[]{:S(2)}) collective-permute-start(f32[1,1,1,224,768]{4,3,2,1,0:T(8,128)} %slice.150), channel_id=1, source_target_pairs={{0,4},{1,5},{2,6},{3,7},{4,8},{5,9},{6,10},{7,11},{8,12},{9,13},{1... | collective-permute-start | bytes 2064392 | tf_op jit(solution)/shard_map/ppermute | solution.py:130
  84.3 3.2 collective-permute-done.7
  88.7 4.1 collective-permute-start.9
  95.1 2.5 constant_dynamic-update-slice_fusion.56
  97.6 9.7 %collective-permute-done.8 = f32[1,1,1,224,768]{4,3,2,1,0:T(8,128)} collective-permute-done((f32[1,1,1,224,768]{4,3,2,1,0:T(8,128)}, f32[1,1,1,224,768]{4,3,2,1,0:T(8,128)}, u32[]{:S(2)}, u32[]{:S(2)}) %collective-permute-start.8) | collective-permute-done | bytes 688160 | tf_op jit(solution)/shard_map/ppermute | solution.py:130
  109.3 7.0 collective-permute-done.9
  117.3 8.1 fusion.19
  128.8 63.3 %collective-permute-done.12 = f32[1,1,1,448,128]{4,3,2,1,0:T(8,128)S(1)} collective-permute-done((f32[1,1,1,448,128]{4,3,2,1,0:T(8,128)S(1)}, f32[1,1,1,448,128]{4,3,2,1,0:T(8,128)S(1)}, u32[]{:S(2)}, u32[]{:S(2)}) %collective-permute-start.12) | collective-permute-done | bytes 229408 | tf_op jit(solution)/shard_map/ppermute | solution.py:130
  195.2 9.3 collective-permute-done.13
  205.9 3.3 collective-permute-start.15
  211.4 19.2 %collective-permute-done.14 = f32[1,2,2,448,128]{4,3,2,1,0:T(8,128)S(1)} collective-permute-done((f32[1,2,2,448,128]{4,3,2,1,0:T(8,128)}, f32[1,2,2,448,128]{4,3,2,1,0:T(8,128)S(1)}, u32[]{:S(2)}, u32[]{:S(2)}) %collective-permute-start.14) | collective-permute-done | bytes 917536 | tf_op jit(solution)/shard_map/ppermute | solution.py:130
  230.7 16.4 %collective-permute-done.15 = f32[1,2,2,448,128]{4,3,2,1,0:T(8,128)S(1)} collective-permute-done((f32[1,2,2,448,128]{4,3,2,1,0:T(8,128)}, f32[1,2,2,448,128]{4,3,2,1,0:T(8,128)S(1)}, u32[]{:S(2)}, u32[]{:S(2)}) %collective-permute-start.15) | collective-permute-done | bytes 917536 | tf_op jit(solution)/shard_map/ppermute | solution.py:130
  247.2 3.8 collective-permute-start.17
  253.0 3.5 constant_dynamic-update-slice_fusion.52
  258.6 3.9 constant_dynamic-update-slice_fusion.49
  265.9 4.4 slice.161
  270.9 5.5 constant_dynamic-update-slice_fusion.36
  276.4 5.4 constant_dynamic-update-slice_fusion.35
  281.8 4.5 slice.162
  295.4 77.8 %collective-permute-done.22 = f32[3,1,2,448,384]{4,3,2,1,0:T(8,128)} collective-permute-done((f32[3,1,2,448,384]{4,3,2,1,0:T(8,128)}, f32[3,1,2,448,384]{4,3,2,1,0:T(8,128)}, u32[]{:S(2)}, u32[]{:S(2)}) %collective-permute-start.22) | collective-permute-done | bytes 4128800 | tf_op jit(solution)/shard_map/ppermute | solution.py:130
  373.2 4.4 constant_dynamic-update-slice_fusion.31
  378.8 4.4 constant_dynamic-update-slice_fusion.30
  383.3 3.9 bitcast_add_fusion.a_ref
  389.1 41.2 %shard_map.48 = (f32[896,896]{1,0:T(8,128)}, f32[896,896]{1,0:T(8,128)}) custom-call(f32[896,896]{1,0:T(8,128)} %bitcast_add_fusion.a_ref, f32[896,896]{1,0:T(8,128)} %broadcast_in_dim.14.done_ref), custom_call_target="tpu_custom_call" | custom-call | flops 20000000000 | bytes 12845056 | tf_op jit(solution)/shard_map/pallas_call | solution.py:90
  430.3 47.2 %shard_map.49 = (f32[896,896]{1,0:T(8,128)}, f32[896,896]{1,0:T(8,128)}) custom-call(f32[896,896]{1,0:T(8,128)} %get-tuple-element.5.a_ref, f32[896,896]{1,0:T(8,128)} %get-tuple-element.6.done_ref), custom_call_target="tpu_custom_call" | custom-call | flops 20000000000 | bytes 12845056 | tf_op jit(solution)/shard_map/pallas_call | solution.py:90
  477.5 8.5 fusion.6
  486.1 6.0 fusion.20
  492.1 27.6 %fusion.2 = f32[448,7168]{1,0:T(8,128)} fusion(f32[7168,896]{1,0:T(8,128)} %bitcast.8, s32[448]{0:T(512)S(1)} %iota_add_fusion, f32[]{:T(128)} %bitcast.2, f32[448,896]{1,0:T(8,128)S(1)} %fusion.20, f32[896,896]{1,0:T(8,128)S(1)} %copy-done.1, s32[]{:T(128)S(6)} %select_n.305, f32[]{:T(128)} %bitcast.4, pred[]{:T(512)} %lt.205, f32[1,448,7168]{2,1,0:T(8,128)} %param.2), kind=kOutput, calls=%fused_computation.5 | convolution fusion | flops 17281015808 | bytes 54593548 | tf_op jit(solution)/shard_map/dot_general | solution.py:21
  522.5 2.9 collective-permute-start.26
  526.2 8.4 collective-permute-done.41
  537.8 18.3 %collective-permute-done.25 = bf16[1,1,1,448,1536]{4,3,2,1,0:T(8,128)(2,1)} collective-permute-done((bf16[1,1,1,448,1536]{4,3,2,1,0:T(8,128)(2,1)}, bf16[1,1,1,448,1536]{4,3,2,1,0:T(8,128)(2,1)}, u32[]{:S(2)}, u32[]{:S(2)}) %collective-permute-start.25) | collective-permute-done | bytes 1376288 | tf_op jit(solution)/shard_map/ppermute | solution.py:130
  560.6 3.8 collective-permute-start.44
  564.5 21.2 %collective-permute-done.26 = bf16[1,1,1,448,1536]{4,3,2,1,0:T(8,128)(2,1)} collective-permute-done((bf16[1,1,1,448,1536]{4,3,2,1,0:T(8,128)(2,1)}, bf16[1,1,1,448,1536]{4,3,2,1,0:T(8,128)(2,1)}, u32[]{:S(2)}, u32[]{:S(2)}) %collective-permute-start.26) | collective-permute-done | bytes 1376288 | tf_op jit(solution)/shard_map/ppermute | solution.py:130
  590.7 9.6 collective-permute-done.27
  600.4 92.0 %collective-permute-done.28 = bf16[1,1,1,224,1536]{4,3,2,1,0:T(8,128)(2,1)S(1)} collective-permute-done((bf16[1,1,1,224,1536]{4,3,2,1,0:T(8,128)(2,1)S(1)}, bf16[1,1,1,224,1536]{4,3,2,1,0:T(8,128)(2,1)S(1)}, u32[]{:S(2)}, u32[]{:S(2)}) %collective-permute-start.28) | collective-permute-done | bytes 688160 | tf_op jit(solution)/shard_map/ppermute | solution.py:130
  692.4 3.0 fusion.18
  699.6 28.9 %collective-permute-done.38 = bf16[4,1,1,448,384]{4,3,2,1,0:T(8,128)(2,1)S(1)} collective-permute-done((bf16[4,1,1,448,384]{4,3,2,1,0:T(8,128)(2,1)S(1)}, bf16[4,1,1,448,384]{4,3,2,1,0:T(8,128)(2,1)S(1)}, u32[]{:S(2)}, u32[]{:S(2)}) %collective-permute-start.38) | collective-permute-done | bytes 1376288 | tf_op jit(solution)/shard_map/ppermute | solution.py:130
  728.8 27.5 %collective-permute-done.35 = bf16[4,1,1,448,384]{4,3,2,1,0:T(8,128)(2,1)S(1)} collective-permute-done((bf16[4,1,1,448,384]{4,3,2,1,0:T(8,128)(2,1)S(1)}, bf16[4,1,1,448,384]{4,3,2,1,0:T(8,128)(2,1)S(1)}, u32[]{:S(2)}, u32[]{:S(2)}) %collective-permute-start.35) | collective-permute-done | bytes 1376288 | tf_op jit(solution)/shard_map/ppermute | solution.py:130
  765.7 11.3 %collective-permute-done.46 = bf16[1,1,2,448,512]{4,3,2,1,0:T(8,128)(2,1)S(1)} collective-permute-done((bf16[1,1,2,448,512]{4,3,2,1,0:T(8,128)(2,1)S(1)}, bf16[1,1,2,448,512]{4,3,2,1,0:T(8,128)(2,1)S(1)}, u32[]{:S(2)}, u32[]{:S(2)}) %collective-permute-start.46) | collective-permute-done | bytes 917536 | tf_op jit(solution)/shard_map/ppermute | solution.py:130
  779.5 3.0 constant_dynamic-update-slice_fusion.4
  782.5 2.9 constant_dynamic-update-slice_fusion.3
  786.7 4.2 constant_dynamic-update-slice_fusion.10
  790.9 3.8 constant_dynamic-update-slice_fusion.14
  794.8 2.5 constant_dynamic-update-slice_fusion.18
  799.3 23.2 %collective-permute-done.39 = bf16[4,2,1,448,384]{4,3,2,1,0:T(8,128)(2,1)} collective-permute-done((bf16[4,2,1,448,384]{4,3,2,1,0:T(8,128)(2,1)}, bf16[4,2,1,448,384]{4,3,2,1,0:T(8,128)(2,1)}, u32[]{:S(2)}, u32[]{:S(2)}) %collective-permute-start.39) | collective-permute-done | bytes 2752544 | tf_op jit(solution)/shard_map/ppermute | solution.py:130
  822.5 2.3 constant_dynamic-update-slice_fusion.9
  824.8 54.2 %collective-permute-done.36 = bf16[4,2,1,448,384]{4,3,2,1,0:T(8,128)(2,1)} collective-permute-done((bf16[4,2,1,448,384]{4,3,2,1,0:T(8,128)(2,1)}, bf16[4,2,1,448,384]{4,3,2,1,0:T(8,128)(2,1)}, u32[]{:S(2)}, u32[]{:S(2)}) %collective-permute-start.36) | collective-permute-done | bytes 2752544 | tf_op jit(solution)/shard_map/ppermute | solution.py:130
  879.0 2.3 constant_dynamic-update-slice_fusion.13
  881.4 4.3 constant_dynamic-update-slice_fusion.17
  885.7 2.4 copy-done.7
  888.2 3.6 constant_dynamic-update-slice_fusion.21
  891.7 19.2 %reduce-precision_convert_fusion = (bf16[448,7168]{1,0:T(8,128)(2,1)}, bf16[448,7168]{1,0:T(8,128)(2,1)}, f32[448,7168]{1,0:T(8,128)}) fusion(f32[448,7168]{1,0:T(8,128)} %fusion.2, f32[448,7168]{1,0:T(8,128)} %collective-permute-done.24), kind=kLoop, calls=%fused_computation.2 | loop fusion | flops 16056320 | bytes 51380224 | tf_op jit(solution)/shard_map/convert_element_type | solution.py:304
  910.9 9.8 %fusion.13 = f32[896,512]{1,0:T(8,128)S(1)} fusion(bf16[7168,512]{1,0:T(8,128)(2,1)S(1)} %bitcast.47, bf16[448,7168]{1,0:T(8,128)(2,1)} %get-tuple-element.11, bf16[448,7168]{1,0:T(8,128)(2,1)} %get-tuple-element.10), kind=kOutput, calls=%fused_computation.103 | convolution fusion | flops 6602358784 | bytes 22020096 | tf_op jit(solution)/shard_map/dot_general | solution.py:307
  921.0 11.6 %fusion.14 = f32[896,384]{1,0:T(8,128)S(1)} fusion(bf16[7168,384]{1,0:T(8,128)(2,1)} %bitcast.60, bf16[448,7168]{1,0:T(8,128)(2,1)} %get-tuple-element.11, bf16[448,7168]{1,0:T(8,128)(2,1)} %get-tuple-element.10), kind=kOutput, calls=%fused_computation.104 | convolution fusion | flops 4958191616 | bytes 19726336 | tf_op jit(solution)/shard_map/dot_general | solution.py:307
  932.6 10.0 %fusion.15 = f32[896,384]{1,0:T(8,128)S(1)} fusion(bf16[7168,384]{1,0:T(8,128)(2,1)} %bitcast.59, bf16[448,7168]{1,0:T(8,128)(2,1)} %get-tuple-element.11, bf16[448,7168]{1,0:T(8,128)(2,1)S(1)} %bitcast.53), kind=kOutput, calls=%fused_computation.105 | convolution fusion | flops 4958191616 | bytes 19726336 | tf_op jit(solution)/shard_map/dot_general | solution.py:307
  942.6 10.2 %fusion.16 = f32[896,384]{1,0:T(8,128)S(1)} fusion(bf16[7168,384]{1,0:T(8,128)(2,1)} %bitcast.56, bf16[448,7168]{1,0:T(8,128)(2,1)} %get-tuple-element.11, bf16[448,7168]{1,0:T(8,128)(2,1)S(1)} %bitcast.53), kind=kOutput, calls=%fused_computation.106 | convolution fusion | flops 4958191616 | bytes 19726336 | tf_op jit(solution)/shard_map/dot_general | solution.py:307
  952.9 10.0 %fusion.17 = f32[896,384]{1,0:T(8,128)S(1)} fusion(bf16[7168,384]{1,0:T(8,128)(2,1)} %bitcast.11, bf16[448,7168]{1,0:T(8,128)(2,1)} %get-tuple-element.11, bf16[448,7168]{1,0:T(8,128)(2,1)S(1)} %bitcast.53), kind=kOutput, calls=%fused_computation.107 | convolution fusion | flops 4958191616 | bytes 19726336 | tf_op jit(solution)/shard_map/dot_general | solution.py:307
  (214 shorter events, 94.2 us)
Async XLA Ops:
  3.8 7.0 collective-permute-start
  6.9 4.5 collective-permute-start.1
  9.5 3.6 collective-permute-start.2
  13.7 3.7 collective-permute-start.3
  15.3 3.6 collective-permute-start.4
  16.7 4.5 collective-permute-start.5
  26.5 35.1 %collective-permute-start.6 = (f32[1,1,1,448,768]{4,3,2,1,0:T(8,128)}, f32[1,1,1,448,768]{4,3,2,1,0:T(8,128)S(1)}, u32[]{:S(2)}, u32[]{:S(2)}) collective-permute-start(f32[1,1,1,448,768]{4,3,2,1,0:T(8,128)} %slice_bitcast_fusion.1), channel_id=1, source_target_pairs={{0,4},{1,5},{2,6},{3,7},{4,8},{5,9},{6,10},{7,11},{8,12},{9,13},{1... | collective-permute-start | bytes 4128776 | tf_op jit(solution)/shard_map/ppermute | solution.py:130
  26.8 60.7 %collective-permute-start.7 = (f32[1,1,1,448,768]{4,3,2,1,0:T(8,128)}, f32[1,1,1,448,768]{4,3,2,1,0:T(8,128)}, u32[]{:S(2)}, u32[]{:S(2)}) collective-permute-start(f32[1,1,1,448,768]{4,3,2,1,0:T(8,128)} %slice_bitcast_fusion.1), channel_id=1, source_target_pairs={{0,12},{1,13},{2,14},{3,15},{4,0},{5,1},{6,2},{7,3},{8,4},{9,5},{1... | collective-permute-start | bytes 4128776 | tf_op jit(solution)/shard_map/ppermute | solution.py:130
  62.5 44.8 %collective-permute-start.8 = (f32[1,1,1,224,768]{4,3,2,1,0:T(8,128)}, f32[1,1,1,224,768]{4,3,2,1,0:T(8,128)}, u32[]{:S(2)}, u32[]{:S(2)}) collective-permute-start(f32[1,1,1,224,768]{4,3,2,1,0:T(8,128)} %slice.150), channel_id=1, source_target_pairs={{0,4},{1,5},{2,6},{3,7},{4,8},{5,9},{6,10},{7,11},{8,12},{9,13},{1... | collective-permute-start | bytes 2064392 | tf_op jit(solution)/shard_map/ppermute | solution.py:130
  88.7 27.7 %collective-permute-start.9 = (f32[1,1,1,224,768]{4,3,2,1,0:T(8,128)S(1)}, f32[1,1,1,224,768]{4,3,2,1,0:T(8,128)S(1)}, u32[]{:S(2)}, u32[]{:S(2)}) collective-permute-start(f32[1,1,1,224,768]{4,3,2,1,0:T(8,128)S(1)} %slice.151), channel_id=1, source_target_pairs={{0,12},{1,13},{2,14},{3,15},{4,0},{5,1},{6,2},{7,3},{8,4},{9,5},{1... | collective-permute-start | bytes 2064392 | tf_op jit(solution)/shard_map/ppermute | solution.py:130
  125.3 127.6 %collective-permute-start.10 = (f32[4,1,1,448,384]{4,3,2,1,0:T(8,128)}, f32[4,1,1,448,384]{4,3,2,1,0:T(8,128)}, u32[]{:S(2)}, u32[]{:S(2)}) collective-permute-start(f32[4,1,1,448,384]{4,3,2,1,0:T(8,128)} %get-tuple-element.28), channel_id=1, source_target_pairs={{0,1},{1,0},{2,3},{3,2},{4,5},{5,4},{6,7},{7,6},{8,9},{9,8},{10,11... | collective-permute-start | bytes 8257544 | tf_op jit(solution)/shard_map/ppermute | solution.py:130
  126.0 132.6 %collective-permute-start.11 = (f32[4,1,1,448,384]{4,3,2,1,0:T(8,128)}, f32[4,1,1,448,384]{4,3,2,1,0:T(8,128)}, u32[]{:S(2)}, u32[]{:S(2)}) collective-permute-start(f32[4,1,1,448,384]{4,3,2,1,0:T(8,128)} %get-tuple-element.25), channel_id=1, source_target_pairs={{0,2},{1,3},{2,0},{3,1},{4,6},{5,7},{6,4},{7,5},{8,10},{9,11},{10,... | collective-permute-start | bytes 8257544 | tf_op jit(solution)/shard_map/ppermute | solution.py:130
  126.5 65.6 %collective-permute-start.12 = (f32[1,1,1,448,128]{4,3,2,1,0:T(8,128)S(1)}, f32[1,1,1,448,128]{4,3,2,1,0:T(8,128)S(1)}, u32[]{:S(2)}, u32[]{:S(2)}) collective-permute-start(f32[1,1,1,448,128]{4,3,2,1,0:T(8,128)S(1)} %slice_bitcast_fusion.3), channel_id=1, source_target_pairs={{0,1},{1,0},{2,3},{3,2},{4,5},{5,4},{6,7},{7,6},{8,9},{9,8},{10,11... | collective-permute-start | bytes 688136 | tf_op jit(solution)/shard_map/ppermute | solution.py:130
  192.8 11.8 %collective-permute-start.13 = (f32[1,1,2,448,128]{4,3,2,1,0:T(8,128)}, f32[1,1,2,448,128]{4,3,2,1,0:T(8,128)S(1)}, u32[]{:S(2)}, u32[]{:S(2)}) collective-permute-start(f32[1,1,2,448,128]{4,3,2,1,0:T(8,128)} %constant_dynamic-update-slice_fusion.46), channel_id=1, source_target_pairs={{0,2},{1,3},{2,0},{3,1},{4,6},{5,7},{6,4},{7,5},{8,10},{9,11},{10,... | collective-permute-start | bytes 1376264 | tf_op jit(solution)/shard_map/ppermute | solution.py:130
  205.4 25.2 %collective-permute-start.14 = (f32[1,2,2,448,128]{4,3,2,1,0:T(8,128)}, f32[1,2,2,448,128]{4,3,2,1,0:T(8,128)S(1)}, u32[]{:S(2)}, u32[]{:S(2)}) collective-permute-start(f32[1,2,2,448,128]{4,3,2,1,0:T(8,128)} %constant_dynamic-update-slice_fusion.44), channel_id=1, source_target_pairs={{0,4},{1,5},{2,6},{3,7},{4,8},{5,9},{6,10},{7,11},{8,12},{9,13},{1... | collective-permute-start | bytes 2752520 | tf_op jit(solution)/shard_map/ppermute | solution.py:130
  205.9 41.2 %collective-permute-start.15 = (f32[1,2,2,448,128]{4,3,2,1,0:T(8,128)}, f32[1,2,2,448,128]{4,3,2,1,0:T(8,128)S(1)}, u32[]{:S(2)}, u32[]{:S(2)}) collective-permute-start(f32[1,2,2,448,128]{4,3,2,1,0:T(8,128)} %constant_dynamic-update-slice_fusion.44), channel_id=1, source_target_pairs={{0,12},{1,13},{2,14},{3,15},{4,0},{5,1},{6,2},{7,3},{8,4},{9,5},{1... | collective-permute-start | bytes 2752520 | tf_op jit(solution)/shard_map/ppermute | solution.py:130
  211.4 45.0 %copy-start.3 = (f32[1,2,2,448,896]{4,3,2,1,0:T(8,128)S(1)}, f32[1,2,2,448,896]{4,3,2,1,0:T(8,128)}, u32[]{:S(2)}) copy-start(f32[1,2,2,448,896]{4,3,2,1,0:T(8,128)} %shard_map.41) | copy-start | bytes 19267588
  230.6 34.0 %collective-permute-start.16 = (f32[1,1,2,448,128]{4,3,2,1,0:T(8,128)S(1)}, f32[1,1,2,448,128]{4,3,2,1,0:T(8,128)S(1)}, u32[]{:S(2)}, u32[]{:S(2)}) collective-permute-start(f32[1,1,2,448,128]{4,3,2,1,0:T(8,128)S(1)} %slice.157), channel_id=1, source_target_pairs={{0,4},{1,5},{2,6},{3,7},{4,8},{5,9},{6,10},{7,11},{8,12},{9,13},{1... | collective-permute-start | bytes 1376264 | tf_op jit(solution)/shard_map/ppermute | solution.py:130
  247.2 18.6 %collective-permute-start.17 = (f32[1,1,2,448,128]{4,3,2,1,0:T(8,128)S(1)}, f32[1,1,2,448,128]{4,3,2,1,0:T(8,128)S(1)}, u32[]{:S(2)}, u32[]{:S(2)}) collective-permute-start(f32[1,1,2,448,128]{4,3,2,1,0:T(8,128)S(1)} %slice.158), channel_id=1, source_target_pairs={{0,12},{1,13},{2,14},{3,15},{4,0},{5,1},{6,2},{7,3},{8,4},{9,5},{1... | collective-permute-start | bytes 1376264 | tf_op jit(solution)/shard_map/ppermute | solution.py:130
  258.0 33.1 %collective-permute-start.18 = (f32[1,1,2,448,384]{4,3,2,1,0:T(8,128)S(1)}, f32[1,1,2,448,384]{4,3,2,1,0:T(8,128)S(1)}, u32[]{:S(2)}, u32[]{:S(2)}) collective-permute-start(f32[1,1,2,448,384]{4,3,2,1,0:T(8,128)S(1)} %get-tuple-element.24), channel_id=1, source_target_pairs={{0,2},{1,3},{2,0},{3,1},{4,6},{5,7},{6,4},{7,5},{8,10},{9,11},{10,... | collective-permute-start | bytes 4128776 | tf_op jit(solution)/shard_map/ppermute | solution.py:130
  264.0 29.2 %collective-permute-start.19 = (f32[1,2,1,448,384]{4,3,2,1,0:T(8,128)S(1)}, f32[1,2,1,448,384]{4,3,2,1,0:T(8,128)S(1)}, u32[]{:S(2)}, u32[]{:S(2)}) collective-permute-start(f32[1,2,1,448,384]{4,3,2,1,0:T(8,128)S(1)} %get-tuple-element.22), channel_id=1, source_target_pairs={{0,1},{1,0},{2,3},{3,2},{4,5},{5,4},{6,7},{7,6},{8,9},{9,8},{10,11... | collective-permute-start | bytes 4128776 | tf_op jit(solution)/shard_map/ppermute | solution.py:130
  270.3 102.9 %collective-permute-start.22 = (f32[3,1,2,448,384]{4,3,2,1,0:T(8,128)}, f32[3,1,2,448,384]{4,3,2,1,0:T(8,128)}, u32[]{:S(2)}, u32[]{:S(2)}) collective-permute-start(f32[3,1,2,448,384]{4,3,2,1,0:T(8,128)} %slice.161), channel_id=1, source_target_pairs={{0,2},{1,3},{2,0},{3,1},{4,6},{5,7},{6,4},{7,5},{8,10},{9,11},{10,... | collective-permute-start | bytes 12386312 | tf_op jit(solution)/shard_map/ppermute | solution.py:130
  286.2 92.6 %collective-permute-start.23 = (f32[3,2,1,448,384]{4,3,2,1,0:T(8,128)}, f32[3,2,1,448,384]{4,3,2,1,0:T(8,128)}, u32[]{:S(2)}, u32[]{:S(2)}) collective-permute-start(f32[3,2,1,448,384]{4,3,2,1,0:T(8,128)} %slice.162), channel_id=1, source_target_pairs={{0,1},{1,0},{2,3},{3,2},{4,5},{5,4},{6,7},{7,6},{8,9},{9,8},{10,11... | collective-permute-start | bytes 12386312 | tf_op jit(solution)/shard_map/ppermute | solution.py:130
  294.8 88.5 %collective-permute-start.20 = (f32[896,896]{1,0:T(8,128)S(1)}, f32[896,896]{1,0:T(8,128)}, u32[]{:S(2)}, u32[]{:S(2)}) collective-permute-start(f32[896,896]{1,0:T(8,128)S(1)} %bitcast.44), channel_id=1, source_target_pairs={{0,16},{16,0},{1,17},{17,1},{2,18},{18,2},{3,19},{19,3},{4,20},{20... | collective-permute-start | bytes 9633800 | tf_op jit(solution)/shard_map/ppermute | solution.py:219
  294.9 182.7 %collective-permute-start.21 = (f32[448,896]{1,0:T(8,128)}, f32[448,896]{1,0:T(8,128)}, u32[]{:S(2)}, u32[]{:S(2)}) collective-permute-start(f32[448,896]{1,0:T(8,128)} %get-tuple-element.8), channel_id=1, source_target_pairs={{0,16},{16,0},{1,17},{17,1},{2,18},{18,2},{3,19},{19,3},{4,20},{20... | collective-permute-start | bytes 4816904 | tf_op jit(solution)/shard_map/ppermute | solution.py:219
  430.3 47.2 %copy-start.6 = (f32[448,896]{1,0:T(8,128)S(1)}, f32[448,896]{1,0:T(8,128)}, u32[]{:S(2)}) copy-start(f32[448,896]{1,0:T(8,128)} %get-tuple-element.8) | copy-start | bytes 4816900
  492.1 27.6 %copy-start.5 = (bf16[1,448,2048]{2,1,0:T(8,128)(2,1)S(1)}, bf16[1,448,2048]{2,1,0:T(8,128)(2,1)}, u32[]{:S(2)}) copy-start(bf16[1,448,2048]{2,1,0:T(8,128)(2,1)} %param.3) | copy-start | bytes 5505028
  519.6 372.1 %collective-permute-start.24 = (f32[448,7168]{1,0:T(8,128)}, f32[448,7168]{1,0:T(8,128)}, u32[]{:S(2)}, u32[]{:S(2)}) collective-permute-start(f32[448,7168]{1,0:T(8,128)} %fusion.2), channel_id=1, source_target_pairs={{0,16},{16,0},{1,17},{17,1},{2,18},{18,2},{3,19},{19,3},{4,20},{20... | collective-permute-start | bytes 38535176 | tf_op jit(solution)/shard_map/ppermute | solution.py:219
  520.9 35.2 %collective-permute-start.25 = (bf16[1,1,1,448,1536]{4,3,2,1,0:T(8,128)(2,1)}, bf16[1,1,1,448,1536]{4,3,2,1,0:T(8,128)(2,1)}, u32[]{:S(2)}, u32[]{:S(2)}) collective-permute-start(bf16[1,1,1,448,1536]{4,3,2,1,0:T(8,128)(2,1)} %slice_bitcast_fusion), channel_id=1, source_target_pairs={{0,4},{1,5},{2,6},{3,7},{4,8},{5,9},{6,10},{7,11},{8,12},{9,13},{1... | collective-permute-start | bytes 4128776 | tf_op jit(solution)/shard_map/ppermute | solution.py:130
  521.9 12.7 %collective-permute-start.41 = (bf16[1,1,1,448,512]{4,3,2,1,0:T(8,128)(2,1)S(1)}, bf16[1,1,1,448,512]{4,3,2,1,0:T(8,128)(2,1)S(1)}, u32[]{:S(2)}, u32[]{:S(2)}) collective-permute-start(bf16[1,1,1,448,512]{4,3,2,1,0:T(8,128)(2,1)S(1)} %slice_bitcast_fusion.2), channel_id=1, source_target_pairs={{0,1},{1,0},{2,3},{3,2},{4,5},{5,4},{6,7},{7,6},{8,9},{9,8},{10,11... | collective-permute-start | bytes 1376264 | tf_op jit(solution)/shard_map/ppermute | solution.py:130
  522.5 63.1 %collective-permute-start.26 = (bf16[1,1,1,448,1536]{4,3,2,1,0:T(8,128)(2,1)}, bf16[1,1,1,448,1536]{4,3,2,1,0:T(8,128)(2,1)}, u32[]{:S(2)}, u32[]{:S(2)}) collective-permute-start(bf16[1,1,1,448,1536]{4,3,2,1,0:T(8,128)(2,1)} %slice_bitcast_fusion), channel_id=1, source_target_pairs={{0,12},{1,13},{2,14},{3,15},{4,0},{5,1},{6,2},{7,3},{8,4},{9,5},{1... | collective-permute-start | bytes 4128776 | tf_op jit(solution)/shard_map/ppermute | solution.py:130
  535.4 22.9 %collective-permute-start.42 = (bf16[1,1,2,448,512]{4,3,2,1,0:T(8,128)(2,1)}, bf16[1,1,2,448,512]{4,3,2,1,0:T(8,128)(2,1)}, u32[]{:S(2)}, u32[]{:S(2)}) collective-permute-start(bf16[1,1,2,448,512]{4,3,2,1,0:T(8,128)(2,1)} %constant_dynamic-update-slice_fusion.7), channel_id=1, source_target_pairs={{0,2},{1,3},{2,0},{3,1},{4,6},{5,7},{6,4},{7,5},{8,10},{9,11},{10,... | collective-permute-start | bytes 2752520 | tf_op jit(solution)/shard_map/ppermute | solution.py:130
  536.6 20.7 %copy-start.15 = (bf16[1,1,2,448,512]{4,3,2,1,0:T(8,128)(2,1)S(1)}, bf16[1,1,2,448,512]{4,3,2,1,0:T(8,128)(2,1)}, u32[]{:S(2)}) copy-start(bf16[1,1,2,448,512]{4,3,2,1,0:T(8,128)(2,1)} %constant_dynamic-update-slice_fusion.7) | copy-start | bytes 2752516
  537.8 49.9 %copy-start = (bf16[4,1,1,448,1536]{4,3,2,1,0:T(8,128)(2,1)S(1)}, bf16[4,1,1,448,1536]{4,3,2,1,0:T(8,128)(2,1)}, u32[]{:S(2)}) copy-start(bf16[4,1,1,448,1536]{4,3,2,1,0:T(8,128)(2,1)} %constant_dynamic-update-slice_fusion.29) | copy-start | bytes 16515076
  557.2 43.1 %collective-permute-start.27 = (bf16[1,1,1,224,1536]{4,3,2,1,0:T(8,128)(2,1)S(1)}, bf16[1,1,1,224,1536]{4,3,2,1,0:T(8,128)(2,1)S(1)}, u32[]{:S(2)}, u32[]{:S(2)}) collective-permute-start(bf16[1,1,1,224,1536]{4,3,2,1,0:T(8,128)(2,1)S(1)} %slice.164), channel_id=1, source_target_pairs={{0,4},{1,5},{2,6},{3,7},{4,8},{5,9},{6,10},{7,11},{8,12},{9,13},{1... | collective-permute-start | bytes 2064392 | tf_op jit(solution)/shard_map/ppermute | solution.py:130
  558.3 134.1 %copy-start.4 = (bf16[4,1,2,448,384]{4,3,2,1,0:T(8,128)(2,1)S(1)}, bf16[4,1,2,448,384]{4,3,2,1,0:T(8,128)(2,1)}, u32[]{:S(2)}) copy-start(bf16[4,1,2,448,384]{4,3,2,1,0:T(8,128)(2,1)} %shard_map.52) | copy-start | bytes 8257540
  560.6 136.8 %collective-permute-start.43 = (bf16[1,2,2,448,512]{4,3,2,1,0:T(8,128)(2,1)}, bf16[1,2,2,448,512]{4,3,2,1,0:T(8,128)(2,1)S(1)}, u32[]{:S(2)}, u32[]{:S(2)}) collective-permute-start(bf16[1,2,2,448,512]{4,3,2,1,0:T(8,128)(2,1)} %constant_dynamic-update-slice_fusion.5), channel_id=1, source_target_pairs={{0,4},{1,5},{2,6},{3,7},{4,8},{5,9},{6,10},{7,11},{8,12},{9,13},{1... | collective-permute-start | bytes 5505032 | tf_op jit(solution)/shard_map/ppermute | solution.py:130
  560.6 138.2 %collective-permute-start.44 = (bf16[1,2,2,448,512]{4,3,2,1,0:T(8,128)(2,1)}, bf16[1,2,2,448,512]{4,3,2,1,0:T(8,128)(2,1)S(1)}, u32[]{:S(2)}, u32[]{:S(2)}) collective-permute-start(bf16[1,2,2,448,512]{4,3,2,1,0:T(8,128)(2,1)} %constant_dynamic-update-slice_fusion.5), channel_id=1, source_target_pairs={{0,12},{1,13},{2,14},{3,15},{4,0},{5,1},{6,2},{7,3},{8,4},{9,5},{1... | collective-permute-start | bytes 5505032 | tf_op jit(solution)/shard_map/ppermute | solution.py:130
  586.8 105.6 %collective-permute-start.28 = (bf16[1,1,1,224,1536]{4,3,2,1,0:T(8,128)(2,1)S(1)}, bf16[1,1,1,224,1536]{4,3,2,1,0:T(8,128)(2,1)S(1)}, u32[]{:S(2)}, u32[]{:S(2)}) collective-permute-start(bf16[1,1,1,224,1536]{4,3,2,1,0:T(8,128)(2,1)S(1)} %slice.165), channel_id=1, source_target_pairs={{0,12},{1,13},{2,14},{3,15},{4,0},{5,1},{6,2},{7,3},{8,4},{9,5},{1... | collective-permute-start | bytes 2064392 | tf_op jit(solution)/shard_map/ppermute | solution.py:130
  695.4 33.1 %collective-permute-start.38 = (bf16[4,1,1,448,384]{4,3,2,1,0:T(8,128)(2,1)S(1)}, bf16[4,1,1,448,384]{4,3,2,1,0:T(8,128)(2,1)S(1)}, u32[]{:S(2)}, u32[]{:S(2)}) collective-permute-start(bf16[4,1,1,448,384]{4,3,2,1,0:T(8,128)(2,1)S(1)} %get-tuple-element.13), channel_id=1, source_target_pairs={{0,2},{1,3},{2,0},{3,1},{4,6},{5,7},{6,4},{7,5},{8,10},{9,11},{10,... | collective-permute-start | bytes 4128776 | tf_op jit(solution)/shard_map/ppermute | solution.py:130
  696.8 59.5 %collective-permute-start.35 = (bf16[4,1,1,448,384]{4,3,2,1,0:T(8,128)(2,1)S(1)}, bf16[4,1,1,448,384]{4,3,2,1,0:T(8,128)(2,1)S(1)}, u32[]{:S(2)}, u32[]{:S(2)}) collective-permute-start(bf16[4,1,1,448,384]{4,3,2,1,0:T(8,128)(2,1)S(1)} %get-tuple-element.18), channel_id=1, source_target_pairs={{0,2},{1,3},{2,0},{3,1},{4,6},{5,7},{6,4},{7,5},{8,10},{9,11},{10,... | collective-permute-start | bytes 4128776 | tf_op jit(solution)/shard_map/ppermute | solution.py:130
  697.5 66.7 %copy-start.11 = (bf16[1,2,2,448,512]{4,3,2,1,0:T(8,128)(2,1)}, bf16[1,2,2,448,512]{4,3,2,1,0:T(8,128)(2,1)S(1)}, u32[]{:S(2)}) copy-start(bf16[1,2,2,448,512]{4,3,2,1,0:T(8,128)(2,1)S(1)} %collective-permute-done.43) | copy-start | bytes 5505028
  697.5 62.1 %collective-permute-start.32 = (bf16[4,1,1,448,384]{4,3,2,1,0:T(8,128)(2,1)S(1)}, bf16[4,1,1,448,384]{4,3,2,1,0:T(8,128)(2,1)S(1)}, u32[]{:S(2)}, u32[]{:S(2)}) collective-permute-start(bf16[4,1,1,448,384]{4,3,2,1,0:T(8,128)(2,1)S(1)} %get-tuple-element.19), channel_id=1, source_target_pairs={{0,1},{1,0},{2,3},{3,2},{4,5},{5,4},{6,7},{7,6},{8,9},{9,8},{10,11... | collective-permute-start | bytes 4128776 | tf_op jit(solution)/shard_map/ppermute | solution.py:130
  698.8 65.3 %copy-start.12 = (bf16[1,2,2,448,512]{4,3,2,1,0:T(8,128)(2,1)}, bf16[1,2,2,448,512]{4,3,2,1,0:T(8,128)(2,1)S(1)}, u32[]{:S(2)}) copy-start(bf16[1,2,2,448,512]{4,3,2,1,0:T(8,128)(2,1)S(1)} %collective-permute-done.44) | copy-start | bytes 5505028
  698.8 62.5 %collective-permute-start.29 = (bf16[4,1,1,448,384]{4,3,2,1,0:T(8,128)(2,1)S(1)}, bf16[4,1,1,448,384]{4,3,2,1,0:T(8,128)(2,1)S(1)}, u32[]{:S(2)}, u32[]{:S(2)}) collective-permute-start(bf16[4,1,1,448,384]{4,3,2,1,0:T(8,128)(2,1)S(1)} %get-tuple-element.20), channel_id=1, source_target_pairs={{0,1},{1,0},{2,3},{3,2},{4,5},{5,4},{6,7},{7,6},{8,9},{9,8},{10,11... | collective-permute-start | bytes 4128776 | tf_op jit(solution)/shard_map/ppermute | solution.py:130
  728.5 35.7 %collective-permute-start.45 = (bf16[1,1,2,448,512]{4,3,2,1,0:T(8,128)(2,1)S(1)}, bf16[1,1,2,448,512]{4,3,2,1,0:T(8,128)(2,1)S(1)}, u32[]{:S(2)}, u32[]{:S(2)}) collective-permute-start(bf16[1,1,2,448,512]{4,3,2,1,0:T(8,128)(2,1)S(1)} %slice.179), channel_id=1, source_target_pairs={{0,4},{1,5},{2,6},{3,7},{4,8},{5,9},{6,10},{7,11},{8,12},{9,13},{1... | collective-permute-start | bytes 2752520 | tf_op jit(solution)/shard_map/ppermute | solution.py:130
  756.3 20.7 %collective-permute-start.46 = (bf16[1,1,2,448,512]{4,3,2,1,0:T(8,128)(2,1)S(1)}, bf16[1,1,2,448,512]{4,3,2,1,0:T(8,128)(2,1)S(1)}, u32[]{:S(2)}, u32[]{:S(2)}) collective-permute-start(bf16[1,1,2,448,512]{4,3,2,1,0:T(8,128)(2,1)S(1)} %slice.180), channel_id=1, source_target_pairs={{0,12},{1,13},{2,14},{3,15},{4,0},{5,1},{6,2},{7,3},{8,4},{9,5},{1... | collective-permute-start | bytes 2752520 | tf_op jit(solution)/shard_map/ppermute | solution.py:130
  759.6 62.9 %collective-permute-start.39 = (bf16[4,2,1,448,384]{4,3,2,1,0:T(8,128)(2,1)}, bf16[4,2,1,448,384]{4,3,2,1,0:T(8,128)(2,1)}, u32[]{:S(2)}, u32[]{:S(2)}) collective-permute-start(bf16[4,2,1,448,384]{4,3,2,1,0:T(8,128)(2,1)} %constant_dynamic-update-slice_fusion.11), channel_id=1, source_target_pairs={{0,1},{1,0},{2,3},{3,2},{4,5},{5,4},{6,7},{7,6},{8,9},{9,8},{10,11... | collective-permute-start | bytes 8257544 | tf_op jit(solution)/shard_map/ppermute | solution.py:130
  761.4 117.6 %collective-permute-start.36 = (bf16[4,2,1,448,384]{4,3,2,1,0:T(8,128)(2,1)}, bf16[4,2,1,448,384]{4,3,2,1,0:T(8,128)(2,1)}, u32[]{:S(2)}, u32[]{:S(2)}) collective-permute-start(bf16[4,2,1,448,384]{4,3,2,1,0:T(8,128)(2,1)} %constant_dynamic-update-slice_fusion.15), channel_id=1, source_target_pairs={{0,1},{1,0},{2,3},{3,2},{4,5},{5,4},{6,7},{7,6},{8,9},{9,8},{10,11... | collective-permute-start | bytes 8257544 | tf_op jit(solution)/shard_map/ppermute | solution.py:130
  764.1 12.8 %copy-start.16 = (bf16[1,1,2,448,512]{4,3,2,1,0:T(8,128)(2,1)}, bf16[1,1,2,448,512]{4,3,2,1,0:T(8,128)(2,1)S(1)}, u32[]{:S(2)}) copy-start(bf16[1,1,2,448,512]{4,3,2,1,0:T(8,128)(2,1)S(1)} %collective-permute-done.45) | copy-start | bytes 2752516
  764.2 117.2 %collective-permute-start.33 = (bf16[4,1,2,448,384]{4,3,2,1,0:T(8,128)(2,1)}, bf16[4,1,2,448,384]{4,3,2,1,0:T(8,128)(2,1)}, u32[]{:S(2)}, u32[]{:S(2)}) collective-permute-start(bf16[4,1,2,448,384]{4,3,2,1,0:T(8,128)(2,1)} %constant_dynamic-update-slice_fusion.19), channel_id=1, source_target_pairs={{0,2},{1,3},{2,0},{3,1},{4,6},{5,7},{6,4},{7,5},{8,10},{9,11},{10,... | collective-permute-start | bytes 8257544 | tf_op jit(solution)/shard_map/ppermute | solution.py:130
  777.9 107.8 %collective-permute-start.30 = (bf16[4,1,2,448,384]{4,3,2,1,0:T(8,128)(2,1)S(1)}, bf16[4,1,2,448,384]{4,3,2,1,0:T(8,128)(2,1)}, u32[]{:S(2)}, u32[]{:S(2)}) collective-permute-start(bf16[4,1,2,448,384]{4,3,2,1,0:T(8,128)(2,1)S(1)} %constant_dynamic-update-slice_fusion.23), channel_id=1, source_target_pairs={{0,2},{1,3},{2,0},{3,1},{4,6},{5,7},{6,4},{7,5},{8,10},{9,11},{10,... | collective-permute-start | bytes 8257544 | tf_op jit(solution)/shard_map/ppermute | solution.py:130
  794.7 84.3 %slice-start.6 = ((s8[5505024]{0:T(1024)(128)(4,1)}), s8[4194304]{0:T(1024)(128)(4,1)S(1)}, s32[]{:S(2)}) async-start(s8[5505024]{0:T(1024)(128)(4,1)} %bitcast.57), calls=%async_computation.6 | async-start | bytes 8388608
  797.2 25.2 %copy-start.9 = (bf16[4,2,2,448,384]{4,3,2,1,0:T(8,128)(2,1)S(1)}, bf16[4,2,2,448,384]{4,3,2,1,0:T(8,128)(2,1)}, u32[]{:S(2)}) copy-start(bf16[4,2,2,448,384]{4,3,2,1,0:T(8,128)(2,1)} %constant_dynamic-update-slice_fusion.10) | copy-start | bytes 16515076
  797.3 81.8 %slice-start.7 = ((s8[5505024]{0:T(1024)(128)(4,1)}), s8[1310720]{0:T(1024)(128)(4,1)S(1)}, s32[]{:S(2)}) async-start(s8[5505024]{0:T(1024)(128)(4,1)} %bitcast.57), calls=%async_computation.7 | async-start | bytes 2621440
  824.8 60.9 %copy-start.10 = (bf16[4,2,2,448,384]{4,3,2,1,0:T(8,128)(2,1)}, bf16[4,2,2,448,384]{4,3,2,1,0:T(8,128)(2,1)S(1)}, u32[]{:S(2)}) copy-start(bf16[4,2,2,448,384]{4,3,2,1,0:T(8,128)(2,1)S(1)} %constant_dynamic-update-slice_fusion.9) | copy-start | bytes 16515076
  881.3 10.4 %copy-start.8 = (bf16[4,2,2,448,384]{4,3,2,1,0:T(8,128)(2,1)}, bf16[4,2,2,448,384]{4,3,2,1,0:T(8,128)(2,1)S(1)}, u32[]{:S(2)}) copy-start(bf16[4,2,2,448,384]{4,3,2,1,0:T(8,128)(2,1)S(1)} %constant_dynamic-update-slice_fusion.13) | copy-start | bytes 16515076
  920.8 11.9 %slice-start.2 = ((s8[6422528]{0:T(1024)(128)(4,1)}), s8[4194304]{0:T(1024)(128)(4,1)S(1)}, s32[]{:S(2)}) async-start(s8[6422528]{0:T(1024)(128)(4,1)} %bitcast.52), calls=%async_computation.2 | async-start | bytes 8388608
  920.9 47.5 %collective-permute-start.47 = (f32[448,512]{1,0:T(8,128)S(1)}, f32[448,512]{1,0:T(8,128)S(1)}, u32[]{:S(2)}, u32[]{:S(2)}) collective-permute-start(f32[448,512]{1,0:T(8,128)S(1)} %slice_add_fusion), channel_id=1, source_target_pairs={{0,16},{16,0},{1,17},{17,1},{2,18},{18,2},{3,19},{19,3},{4,20},{20... | collective-permute-start | bytes 2752520 | tf_op jit(solution)/shard_map/ppermute | solution.py:219
  921.0 11.6 %slice-start.3 = ((s8[6422528]{0:T(1024)(128)(4,1)}), s8[2228224]{0:T(1024)(128)(4,1)S(1)}, s32[]{:S(2)}) async-start(s8[6422528]{0:T(1024)(128)(4,1)} %bitcast.52), calls=%async_computation.3 | async-start | bytes 4456448
  963.0 2.3 collective-permute-start.31
  963.6 2.7 collective-permute-start.34
  963.8 3.5 collective-permute-start.37
  964.4 3.9 collective-permute-start.40
  (13 other events, 74.0 us)

commit v2 on v1

--- a/solution.py
+++ b/solution.py
@@ -20,6 +20,23 @@
 def dot(a, b, dims, precision):
     return lax.dot_general(
         a, b, (dims, ((), ())), precision=precision, preferred_element_type=jnp.float32
+    )
+
+
+def parts(value):
+    high = value.astype(jnp.bfloat16).astype(jnp.float32)
+    rest = value - high
+    mid = rest.astype(jnp.bfloat16).astype(jnp.float32)
+    return high, mid, rest - mid
+
+
+def rank_update(left, right):
+    high, mid, low = parts(left)
+    left = jnp.concatenate([high, high, mid, high, mid, low], axis=0).astype(jnp.bfloat16)
+    high, mid, low = parts(right)
+    right = jnp.concatenate([high, mid, high, low, mid, high], axis=0).astype(jnp.bfloat16)
+    return lax.dot_general(
+        left, right, (((0,), (0,)), ((), ())), preferred_element_type=jnp.float32
     )
 
 
@@ -41,7 +58,6 @@
         for i in range(GROUP):
             pivot = small[i, i]
             root = lax.rsqrt(pivot)
-            root = root * (1.5 - 0.5 * pivot * root * root)
             us[i] = us[i] * root
             xs[i] = xs[i] * root
             ratio = {k: small[i, k] * root for k in range(i + 1, GROUP)}
@@ -53,8 +69,9 @@
         u = jnp.concatenate(us, axis=0)
         x = jnp.concatenate(xs, axis=0)
         left = jnp.where(lanes < BLOCK - GROUP * step, u, 0.0)
-        d_new = d_ref[GROUP:, :] - dot(left, u, ((0,), (0,)), EXACT)[GROUP:, :]
-        x_new = x_ref[GROUP:, :] - dot(left, x, ((0,), (0,)), EXACT)[GROUP:, :]
+        gone = rank_update(left, jnp.concatenate([u, x], axis=1))
+        d_new = d_ref[GROUP:, :] - gone[GROUP:, :BLOCK]
+        x_new = x_ref[GROUP:, :] - gone[GROUP:, BLOCK:]
         d_ref[0 : BLOCK - GROUP, :] = pltpu.roll(d_new, BLOCK - GROUP, 1)
         d_ref[BLOCK - GROUP :, :] = jnp.zeros((GROUP, BLOCK), jnp.float32)
         x_ref[0 : BLOCK - GROUP, :] = x_new
@@ -287,7 +304,7 @@
 
     corner = scaling * plane.reshape(-1, panel)[:panel]
     corner = corner + swapped(corner)
-    own = scaling * own_panel
+    own = scaling * after(own_panel, early[:1, :1, :1, :8, :128])
     own = own + swapped(own)
     inverse = inverse_factor(corner)
     factored = position < PANEL_STEPS

time: 979 us -> 1000 us (1.021)
  waiting for transfers between devices: 546 us -> 607 us
  starting transfers between devices: 77.7 us -> 48.8 us
  Pallas kernels: 88.5 us -> 71.4 us
  local copies, waits for them, and re-layouts: 132 us -> 142 us
    ppermute x6, waiting for transfers between devices: 6.2 us -> 50 us  [torus_sum(): total = total + lax.ppermute(value, 'row', pairs)]
    ppermute x34, starting transfers between devices: 65.2 us -> 41.5 us  [shifted(): return lax.ppermute(value, 'row', pairs)]
    pallas_call x2, Pallas kernels: 88.5 us -> 71.4 us  [eliminate(): pl.pallas_call(functools.partial(factor_body, blocks), out_shape=(whole,...]
    ppermute x34, waiting for transfers between devices: 537 us -> 553 us  [shifted(): return lax.ppermute(value, 'row', pairs)]
  transfers between devices with their start and end apart: 48 -> 48, of which waited for: 32 -> 31; matrix products, arithmetic and copies ran while one was open for 17% -> 18% of each run, Pallas kernels for 9% -> 7%
where the time goes in v2:
time: 1000 us; the launch traced here: 996 us
  waiting for transfers between devices  607 us (61%)
  local copies, waits for them, and re-layouts  142 us (14%)
  matrix products  93.1 us (9%)
  Pallas kernels  71.4 us (7%)
  starting transfers between devices  48.8 us (5%)
  other arithmetic  32.4 us (3%)
    ppermute x34, waiting for transfers between devices, shifted(): return lax.ppermute(value, 'row', pairs)  553 us
    dynamic_update_slice x52, local copies, waits for them, and re-layouts, fill(): lax.dynamic_update_slice(buffer, chunk, tuple((jnp.asarray(i, jnp.int32)...  102 us
    pallas_call x2, Pallas kernels, eliminate(): pl.pallas_call(functools.partial(factor_body, blocks), out_shape=(whole,...  71.4 us
    dot_general x5, matrix products, per_device(): part = jnp.dot(both, weight, preferred_element_type=jnp.float32)  51.7 us
    ppermute x6, waiting for transfers between devices, torus_sum(): total = total + lax.ppermute(value, 'row', pairs)  50 us
    dot_general x3, matrix products, dot(): lax.dot_general(a, b, (dims, ((), ())), precision=precision, preferred_el...  41.5 us
    ppermute x34, starting transfers between devices, shifted(): return lax.ppermute(value, 'row', pairs)  41.5 us
  transfers between devices with their start and end apart: 48, of which 31 were waited for; matrix products, arithmetic and copies ran while one was open for 18% of the time, Pallas kernels for 7%

profile of v2, /device:TPU:0, one launch (start us, length us, event | category | flops | bytes accessed | tf_op | source)
XLA Modules:
  0.0 996.5 jit_solution(14880358911207592407)
XLA Ops:
  3.5 3.1 collective-permute-start.6
  8.6 31.3 %collective-permute-done.6 = f32[1,1,1,448,768]{4,3,2,1,0:T(8,128)S(1)} collective-permute-done((f32[1,1,1,448,768]{4,3,2,1,0:T(8,128)}, f32[1,1,1,448,768]{4,3,2,1,0:T(8,128)S(1)}, u32[]{:S(2)}, u32[]{:S(2)}) %collective-permute-start.6) | collective-permute-done | bytes 1376288 | tf_op jit(solution)/shard_map/ppermute | solution.py:147
  40.8 27.5 %collective-permute-done.7 = f32[1,1,1,448,768]{4,3,2,1,0:T(8,128)} collective-permute-done((f32[1,1,1,448,768]{4,3,2,1,0:T(8,128)}, f32[1,1,1,448,768]{4,3,2,1,0:T(8,128)}, u32[]{:S(2)}, u32[]{:S(2)}) %collective-permute-start.7) | collective-permute-done | bytes 1376288 | tf_op jit(solution)/shard_map/ppermute | solution.py:147
  69.4 3.1 collective-permute-start.9
  74.8 2.5 constant_dynamic-update-slice_fusion.56
  77.3 9.7 collective-permute-done.8
  89.0 9.0 collective-permute-done.9
  98.9 8.1 fusion.19
  111.3 62.4 %collective-permute-done.12 = f32[1,1,1,448,128]{4,3,2,1,0:T(8,128)S(1)} collective-permute-done((f32[1,1,1,448,128]{4,3,2,1,0:T(8,128)S(1)}, f32[1,1,1,448,128]{4,3,2,1,0:T(8,128)S(1)}, u32[]{:S(2)}, u32[]{:S(2)}) %collective-permute-start.12) | collective-permute-done | bytes 229408 | tf_op jit(solution)/shard_map/ppermute | solution.py:147
  177.8 8.5 collective-permute-done.13
  187.6 3.3 collective-permute-start.15
  190.9 2.4 fusion.9
  194.0 35.4 %collective-permute-done = f32[8,128]{1,0:T(8,128)S(1)} collective-permute-done((f32[8,128]{1,0:T(8,128)S(1)}, f32[8,128]{1,0:T(8,128)S(1)}, u32[]{:S(2)}, u32[]{:S(2)}) %collective-permute-start) | collective-permute-done | bytes 4128 | tf_op jit(solution)/shard_map/ppermute | solution.py:227
  229.5 4.5 collective-permute-done.1
  234.0 3.6 collective-permute-done.2
  245.5 2.4 collective-permute-start.5
  253.4 3.7 collective-permute-start.17
  260.3 3.5 constant_dynamic-update-slice_fusion.52
  266.9 3.5 constant_dynamic-update-slice_fusion.49
  273.6 4.4 slice.166
  278.8 5.5 constant_dynamic-update-slice_fusion.36
  284.2 5.5 constant_dynamic-update-slice_fusion.35
  289.7 4.5 slice.167
  294.8 2.3 constant_dynamic-update-slice_fusion.34
  299.8 3.0 collective-permute-done.19
  306.6 70.6 %collective-permute-done.22 = f32[3,1,2,448,384]{4,3,2,1,0:T(8,128)} collective-permute-done((f32[3,1,2,448,384]{4,3,2,1,0:T(8,128)}, f32[3,1,2,448,384]{4,3,2,1,0:T(8,128)}, u32[]{:S(2)}, u32[]{:S(2)}) %collective-permute-start.22) | collective-permute-done | bytes 4128800 | tf_op jit(solution)/shard_map/ppermute | solution.py:147
  377.2 4.4 constant_dynamic-update-slice_fusion.31
  383.5 4.5 constant_dynamic-update-slice_fusion.30
  388.1 4.9 bitcast_add_fusion.a_ref
  394.8 34.0 %shard_map.48 = (f32[896,896]{1,0:T(8,128)}, f32[896,896]{1,0:T(8,128)}) custom-call(f32[896,896]{1,0:T(8,128)} %bitcast_add_fusion.a_ref, f32[896,896]{1,0:T(8,128)} %broadcast_in_dim.14.done_ref), custom_call_target="tpu_custom_call" | custom-call | flops 20000000000 | bytes 12845056 | tf_op jit(solution)/shard_map/pallas_call | solution.py:107
  428.8 37.4 %shard_map.49 = (f32[896,896]{1,0:T(8,128)}, f32[896,896]{1,0:T(8,128)}) custom-call(f32[896,896]{1,0:T(8,128)} %get-tuple-element.7.a_ref, f32[896,896]{1,0:T(8,128)} %get-tuple-element.8.done_ref), custom_call_target="tpu_custom_call" | custom-call | flops 20000000000 | bytes 12845056 | tf_op jit(solution)/shard_map/pallas_call | solution.py:107
  466.3 8.0 fusion.6
  474.3 5.9 fusion.20
  480.2 27.5 %fusion.2 = f32[448,7168]{1,0:T(8,128)} fusion(f32[7168,896]{1,0:T(8,128)} %bitcast.8, s32[448]{0:T(512)S(1)} %iota_add_fusion, f32[]{:T(128)} %bitcast.2, f32[448,896]{1,0:T(8,128)S(1)} %fusion.20, f32[896,896]{1,0:T(8,128)S(1)} %copy-done, s32[]{:T(128)S(6)} %select_n.305, f32[]{:T(128)} %bitcast.4, pred[]{:T(512)} %lt.205, f32[1,448,7168]{2,1,0:T(8,128)} %param.2), kind=kOutput, calls=%fused_computation.5 | convolution fusion | flops 17281015808 | bytes 54593548 | tf_op jit(solution)/shard_map/dot_general | solution.py:21
  510.2 10.6 %collective-permute-done.41 = bf16[1,1,1,448,512]{4,3,2,1,0:T(8,128)(2,1)S(1)} collective-permute-done((bf16[1,1,1,448,512]{4,3,2,1,0:T(8,128)(2,1)S(1)}, bf16[1,1,1,448,512]{4,3,2,1,0:T(8,128)(2,1)S(1)}, u32[]{:S(2)}, u32[]{:S(2)}) %collective-permute-start.41) | collective-permute-done | bytes 458784 | tf_op jit(solution)/shard_map/ppermute | solution.py:147
  525.7 18.2 %collective-permute-done.42 = bf16[1,1,2,448,512]{4,3,2,1,0:T(8,128)(2,1)} collective-permute-done((bf16[1,1,2,448,512]{4,3,2,1,0:T(8,128)(2,1)}, bf16[1,1,2,448,512]{4,3,2,1,0:T(8,128)(2,1)}, u32[]{:S(2)}, u32[]{:S(2)}) %collective-permute-start.42) | collective-permute-done | bytes 917536 | tf_op jit(solution)/shard_map/ppermute | solution.py:147
  546.0 3.8 collective-permute-start.26
  549.9 11.0 %collective-permute-done.25 = bf16[1,1,1,448,1536]{4,3,2,1,0:T(8,128)(2,1)S(1)} collective-permute-done((bf16[1,1,1,448,1536]{4,3,2,1,0:T(8,128)(2,1)}, bf16[1,1,1,448,1536]{4,3,2,1,0:T(8,128)(2,1)S(1)}, u32[]{:S(2)}, u32[]{:S(2)}) %collective-permute-start.25) | collective-permute-done | bytes 1376288 | tf_op jit(solution)/shard_map/ppermute | solution.py:147
  562.2 38.0 %collective-permute-done.43 = bf16[1,2,2,448,512]{4,3,2,1,0:T(8,128)(2,1)} collective-permute-done((bf16[1,2,2,448,512]{4,3,2,1,0:T(8,128)(2,1)}, bf16[1,2,2,448,512]{4,3,2,1,0:T(8,128)(2,1)}, u32[]{:S(2)}, u32[]{:S(2)}) %collective-permute-start.43) | collective-permute-done | bytes 1835040 | tf_op jit(solution)/shard_map/ppermute | solution.py:147
  601.5 26.7 %collective-permute-done.26 = bf16[1,1,1,448,1536]{4,3,2,1,0:T(8,128)(2,1)} collective-permute-done((bf16[1,1,1,448,1536]{4,3,2,1,0:T(8,128)(2,1)}, bf16[1,1,1,448,1536]{4,3,2,1,0:T(8,128)(2,1)}, u32[]{:S(2)}, u32[]{:S(2)}) %collective-permute-start.26) | collective-permute-done | bytes 1376288 | tf_op jit(solution)/shard_map/ppermute | solution.py:147
  632.1 2.5 constant_dynamic-update-slice_fusion.27
  634.6 49.2 %collective-permute-done.27 = bf16[1,1,1,224,1536]{4,3,2,1,0:T(8,128)(2,1)S(1)} collective-permute-done((bf16[1,1,1,224,1536]{4,3,2,1,0:T(8,128)(2,1)S(1)}, bf16[1,1,1,224,1536]{4,3,2,1,0:T(8,128)(2,1)S(1)}, u32[]{:S(2)}, u32[]{:S(2)}) %collective-permute-start.27) | collective-permute-done | bytes 688160 | tf_op jit(solution)/shard_map/ppermute | solution.py:147
  684.7 31.8 %collective-permute-done.28 = bf16[1,1,1,224,1536]{4,3,2,1,0:T(8,128)(2,1)S(1)} collective-permute-done((bf16[1,1,1,224,1536]{4,3,2,1,0:T(8,128)(2,1)S(1)}, bf16[1,1,1,224,1536]{4,3,2,1,0:T(8,128)(2,1)S(1)}, u32[]{:S(2)}, u32[]{:S(2)}) %collective-permute-start.28) | collective-permute-done | bytes 688160 | tf_op jit(solution)/shard_map/ppermute | solution.py:147
  717.4 5.2 fusion.18
  726.7 28.9 %collective-permute-done.38 = bf16[4,1,1,448,384]{4,3,2,1,0:T(8,128)(2,1)S(1)} collective-permute-done((bf16[4,1,1,448,384]{4,3,2,1,0:T(8,128)(2,1)S(1)}, bf16[4,1,1,448,384]{4,3,2,1,0:T(8,128)(2,1)S(1)}, u32[]{:S(2)}, u32[]{:S(2)}) %collective-permute-start.38) | collective-permute-done | bytes 1376288 | tf_op jit(solution)/shard_map/ppermute | solution.py:147
  757.2 27.1 %collective-permute-done.35 = bf16[4,1,1,448,384]{4,3,2,1,0:T(8,128)(2,1)S(1)} collective-permute-done((bf16[4,1,1,448,384]{4,3,2,1,0:T(8,128)(2,1)S(1)}, bf16[4,1,1,448,384]{4,3,2,1,0:T(8,128)(2,1)S(1)}, u32[]{:S(2)}, u32[]{:S(2)}) %collective-permute-start.35) | collective-permute-done | bytes 1376288 | tf_op jit(solution)/shard_map/ppermute | solution.py:147
  795.9 3.0 constant_dynamic-update-slice_fusion.3
  802.3 4.2 constant_dynamic-update-slice_fusion.10
  806.5 2.5 constant_dynamic-update-slice_fusion.14
  809.0 2.4 constant_dynamic-update-slice_fusion.18
  811.4 3.6 constant_dynamic-update-slice_fusion.22
  815.0 32.0 %collective-permute-done.39 = bf16[4,2,1,448,384]{4,3,2,1,0:T(8,128)(2,1)} collective-permute-done((bf16[4,2,1,448,384]{4,3,2,1,0:T(8,128)(2,1)}, bf16[4,2,1,448,384]{4,3,2,1,0:T(8,128)(2,1)}, u32[]{:S(2)}, u32[]{:S(2)}) %collective-permute-start.39) | collective-permute-done | bytes 2752544 | tf_op jit(solution)/shard_map/ppermute | solution.py:147
  847.1 2.3 constant_dynamic-update-slice_fusion.9
  849.4 54.8 %collective-permute-done.36 = bf16[4,2,1,448,384]{4,3,2,1,0:T(8,128)(2,1)} collective-permute-done((bf16[4,2,1,448,384]{4,3,2,1,0:T(8,128)(2,1)}, bf16[4,2,1,448,384]{4,3,2,1,0:T(8,128)(2,1)}, u32[]{:S(2)}, u32[]{:S(2)}) %collective-permute-start.36) | collective-permute-done | bytes 2752544 | tf_op jit(solution)/shard_map/ppermute | solution.py:147
  904.3 2.3 constant_dynamic-update-slice_fusion.13
  906.6 4.3 constant_dynamic-update-slice_fusion.17
  910.9 2.4 copy-done.5
  913.3 3.7 constant_dynamic-update-slice_fusion.21
  917.0 19.3 %reduce-precision_convert_fusion = (bf16[448,7168]{1,0:T(8,128)(2,1)}, bf16[448,7168]{1,0:T(8,128)(2,1)}, f32[448,7168]{1,0:T(8,128)}) fusion(f32[448,7168]{1,0:T(8,128)} %fusion.2, f32[448,7168]{1,0:T(8,128)} %collective-permute-done.24), kind=kLoop, calls=%fused_computation.2 | loop fusion | flops 16056320 | bytes 51380224 | tf_op jit(solution)/shard_map/convert_element_type | solution.py:321
  936.4 9.8 fusion.13
  946.5 11.6 %fusion.14 = f32[896,384]{1,0:T(8,128)S(1)} fusion(bf16[7168,384]{1,0:T(8,128)(2,1)} %bitcast.61, bf16[448,7168]{1,0:T(8,128)(2,1)} %get-tuple-element.13, bf16[448,7168]{1,0:T(8,128)(2,1)} %get-tuple-element.12), kind=kOutput, calls=%fused_computation.104 | convolution fusion | flops 4958191616 | bytes 19726336 | tf_op jit(solution)/shard_map/dot_general | solution.py:324
  958.1 10.0 %fusion.15 = f32[896,384]{1,0:T(8,128)S(1)} fusion(bf16[7168,384]{1,0:T(8,128)(2,1)} %bitcast.58, bf16[448,7168]{1,0:T(8,128)(2,1)} %get-tuple-element.13, bf16[448,7168]{1,0:T(8,128)(2,1)S(1)} %bitcast.52), kind=kOutput, calls=%fused_computation.105 | convolution fusion | flops 4958191616 | bytes 19726336 | tf_op jit(solution)/shard_map/dot_general | solution.py:324
  968.1 10.3 %fusion.16 = f32[896,384]{1,0:T(8,128)S(1)} fusion(bf16[7168,384]{1,0:T(8,128)(2,1)} %bitcast.55, bf16[448,7168]{1,0:T(8,128)(2,1)} %get-tuple-element.13, bf16[448,7168]{1,0:T(8,128)(2,1)S(1)} %bitcast.52), kind=kOutput, calls=%fused_computation.106 | convolution fusion | flops 4958191616 | bytes 19726336 | tf_op jit(solution)/shard_map/dot_general | solution.py:324
  978.4 10.0 %fusion.17 = f32[896,384]{1,0:T(8,128)S(1)} fusion(bf16[7168,384]{1,0:T(8,128)(2,1)} %bitcast.11, bf16[448,7168]{1,0:T(8,128)(2,1)} %get-tuple-element.13, bf16[448,7168]{1,0:T(8,128)(2,1)S(1)} %bitcast.52), kind=kOutput, calls=%fused_computation.107 | convolution fusion | flops 4958191616 | bytes 19726336 | tf_op jit(solution)/shard_map/dot_general | solution.py:324
  (210 shorter events, 102.8 us)
Async XLA Ops:
  3.5 36.4 %collective-permute-start.6 = (f32[1,1,1,448,768]{4,3,2,1,0:T(8,128)}, f32[1,1,1,448,768]{4,3,2,1,0:T(8,128)S(1)}, u32[]{:S(2)}, u32[]{:S(2)}) collective-permute-start(f32[1,1,1,448,768]{4,3,2,1,0:T(8,128)} %slice_bitcast_fusion), channel_id=1, source_target_pairs={{0,4},{1,5},{2,6},{3,7},{4,8},{5,9},{6,10},{7,11},{8,12},{9,13},{1... | collective-permute-start | bytes 4128776 | tf_op jit(solution)/shard_map/ppermute | solution.py:147
  6.6 61.7 %collective-permute-start.7 = (f32[1,1,1,448,768]{4,3,2,1,0:T(8,128)}, f32[1,1,1,448,768]{4,3,2,1,0:T(8,128)}, u32[]{:S(2)}, u32[]{:S(2)}) collective-permute-start(f32[1,1,1,448,768]{4,3,2,1,0:T(8,128)} %slice_bitcast_fusion), channel_id=1, source_target_pairs={{0,12},{1,13},{2,14},{3,15},{4,0},{5,1},{6,2},{7,3},{8,4},{9,5},{1... | collective-permute-start | bytes 4128776 | tf_op jit(solution)/shard_map/ppermute | solution.py:147
  40.8 46.3 %collective-permute-start.8 = (f32[1,1,1,224,768]{4,3,2,1,0:T(8,128)}, f32[1,1,1,224,768]{4,3,2,1,0:T(8,128)}, u32[]{:S(2)}, u32[]{:S(2)}) collective-permute-start(f32[1,1,1,224,768]{4,3,2,1,0:T(8,128)} %slice.154), channel_id=1, source_target_pairs={{0,4},{1,5},{2,6},{3,7},{4,8},{5,9},{6,10},{7,11},{8,12},{9,13},{1... | collective-permute-start | bytes 2064392 | tf_op jit(solution)/shard_map/ppermute | solution.py:147
  69.4 28.6 %collective-permute-start.9 = (f32[1,1,1,224,768]{4,3,2,1,0:T(8,128)S(1)}, f32[1,1,1,224,768]{4,3,2,1,0:T(8,128)S(1)}, u32[]{:S(2)}, u32[]{:S(2)}) collective-permute-start(f32[1,1,1,224,768]{4,3,2,1,0:T(8,128)S(1)} %slice.155), channel_id=1, source_target_pairs={{0,12},{1,13},{2,14},{3,15},{4,0},{5,1},{6,2},{7,3},{8,4},{9,5},{1... | collective-permute-start | bytes 2064392 | tf_op jit(solution)/shard_map/ppermute | solution.py:147
  107.0 153.3 %collective-permute-start.10 = (f32[4,1,1,448,384]{4,3,2,1,0:T(8,128)}, f32[4,1,1,448,384]{4,3,2,1,0:T(8,128)}, u32[]{:S(2)}, u32[]{:S(2)}) collective-permute-start(f32[4,1,1,448,384]{4,3,2,1,0:T(8,128)} %get-tuple-element.30), channel_id=1, source_target_pairs={{0,1},{1,0},{2,3},{3,2},{4,5},{5,4},{6,7},{7,6},{8,9},{9,8},{10,11... | collective-permute-start | bytes 8257544 | tf_op jit(solution)/shard_map/ppermute | solution.py:147
  108.4 158.4 %collective-permute-start.11 = (f32[4,1,1,448,384]{4,3,2,1,0:T(8,128)}, f32[4,1,1,448,384]{4,3,2,1,0:T(8,128)}, u32[]{:S(2)}, u32[]{:S(2)}) collective-permute-start(f32[4,1,1,448,384]{4,3,2,1,0:T(8,128)} %get-tuple-element.27), channel_id=1, source_target_pairs={{0,2},{1,3},{2,0},{3,1},{4,6},{5,7},{6,4},{7,5},{8,10},{9,11},{10,... | collective-permute-start | bytes 8257544 | tf_op jit(solution)/shard_map/ppermute | solution.py:147
  110.0 63.7 %collective-permute-start.12 = (f32[1,1,1,448,128]{4,3,2,1,0:T(8,128)S(1)}, f32[1,1,1,448,128]{4,3,2,1,0:T(8,128)S(1)}, u32[]{:S(2)}, u32[]{:S(2)}) collective-permute-start(f32[1,1,1,448,128]{4,3,2,1,0:T(8,128)S(1)} %slice_bitcast_fusion.3), channel_id=1, source_target_pairs={{0,1},{1,0},{2,3},{3,2},{4,5},{5,4},{6,7},{7,6},{8,9},{9,8},{10,11... | collective-permute-start | bytes 688136 | tf_op jit(solution)/shard_map/ppermute | solution.py:147
  174.4 11.8 %collective-permute-start.13 = (f32[1,1,2,448,128]{4,3,2,1,0:T(8,128)}, f32[1,1,2,448,128]{4,3,2,1,0:T(8,128)S(1)}, u32[]{:S(2)}, u32[]{:S(2)}) collective-permute-start(f32[1,1,2,448,128]{4,3,2,1,0:T(8,128)} %constant_dynamic-update-slice_fusion.46), channel_id=1, source_target_pairs={{0,2},{1,3},{2,0},{3,1},{4,6},{5,7},{6,4},{7,5},{8,10},{9,11},{10,... | collective-permute-start | bytes 1376264 | tf_op jit(solution)/shard_map/ppermute | solution.py:147
  187.1 65.1 %collective-permute-start.14 = (f32[1,2,2,448,128]{4,3,2,1,0:T(8,128)}, f32[1,2,2,448,128]{4,3,2,1,0:T(8,128)S(1)}, u32[]{:S(2)}, u32[]{:S(2)}) collective-permute-start(f32[1,2,2,448,128]{4,3,2,1,0:T(8,128)} %constant_dynamic-update-slice_fusion.44), channel_id=1, source_target_pairs={{0,4},{1,5},{2,6},{3,7},{4,8},{5,9},{6,10},{7,11},{8,12},{9,13},{1... | collective-permute-start | bytes 2752520 | tf_op jit(solution)/shard_map/ppermute | solution.py:147
  187.6 64.6 %collective-permute-start.15 = (f32[1,2,2,448,128]{4,3,2,1,0:T(8,128)}, f32[1,2,2,448,128]{4,3,2,1,0:T(8,128)}, u32[]{:S(2)}, u32[]{:S(2)}) collective-permute-start(f32[1,2,2,448,128]{4,3,2,1,0:T(8,128)} %constant_dynamic-update-slice_fusion.44), channel_id=1, source_target_pairs={{0,12},{1,13},{2,14},{3,15},{4,0},{5,1},{6,2},{7,3},{8,4},{9,5},{1... | collective-permute-start | bytes 2752520 | tf_op jit(solution)/shard_map/ppermute | solution.py:147
  194.0 35.5 %collective-permute-start = (f32[8,128]{1,0:T(8,128)S(1)}, f32[8,128]{1,0:T(8,128)S(1)}, u32[]{:S(2)}, u32[]{:S(2)}) collective-permute-start(f32[8,128]{1,0:T(8,128)S(1)} %broadcast_in_dim.13), channel_id=1, source_target_pairs={{0,4},{1,5},{2,6},{3,7},{4,8},{5,9},{6,10},{7,11},{8,12},{9,13},{1... | collective-permute-start | bytes 12296 | tf_op jit(solution)/shard_map/ppermute | solution.py:227
  229.5 4.5 collective-permute-start.1
  234.0 3.6 collective-permute-start.2
  238.2 3.7 collective-permute-start.3
  241.9 3.6 collective-permute-start.4
  245.5 4.5 collective-permute-start.5
  252.1 11.7 %copy-start.2 = (f32[1,2,2,448,896]{4,3,2,1,0:T(8,128)S(1)}, f32[1,2,2,448,896]{4,3,2,1,0:T(8,128)}, u32[]{:S(2)}) copy-start(f32[1,2,2,448,896]{4,3,2,1,0:T(8,128)} %shard_map.41) | copy-start | bytes 19267588
  252.2 21.4 %collective-permute-start.16 = (f32[1,1,2,448,128]{4,3,2,1,0:T(8,128)S(1)}, f32[1,1,2,448,128]{4,3,2,1,0:T(8,128)S(1)}, u32[]{:S(2)}, u32[]{:S(2)}) collective-permute-start(f32[1,1,2,448,128]{4,3,2,1,0:T(8,128)S(1)} %slice.161), channel_id=1, source_target_pairs={{0,4},{1,5},{2,6},{3,7},{4,8},{5,9},{6,10},{7,11},{8,12},{9,13},{1... | collective-permute-start | bytes 1376264 | tf_op jit(solution)/shard_map/ppermute | solution.py:147
  253.4 20.1 %collective-permute-start.17 = (f32[1,1,2,448,128]{4,3,2,1,0:T(8,128)S(1)}, f32[1,1,2,448,128]{4,3,2,1,0:T(8,128)S(1)}, u32[]{:S(2)}, u32[]{:S(2)}) collective-permute-start(f32[1,1,2,448,128]{4,3,2,1,0:T(8,128)S(1)} %slice.162), channel_id=1, source_target_pairs={{0,12},{1,13},{2,14},{3,15},{4,0},{5,1},{6,2},{7,3},{8,4},{9,5},{1... | collective-permute-start | bytes 1376264 | tf_op jit(solution)/shard_map/ppermute | solution.py:147
  265.3 8.2 copy-start.1
  265.3 33.1 %collective-permute-start.18 = (f32[1,1,2,448,384]{4,3,2,1,0:T(8,128)S(1)}, f32[1,1,2,448,384]{4,3,2,1,0:T(8,128)S(1)}, u32[]{:S(2)}, u32[]{:S(2)}) collective-permute-start(f32[1,1,2,448,384]{4,3,2,1,0:T(8,128)S(1)} %get-tuple-element.26), channel_id=1, source_target_pairs={{0,2},{1,3},{2,0},{3,1},{4,6},{5,7},{6,4},{7,5},{8,10},{9,11},{10,... | collective-permute-start | bytes 4128776 | tf_op jit(solution)/shard_map/ppermute | solution.py:147
  271.9 30.8 %collective-permute-start.19 = (f32[1,2,1,448,384]{4,3,2,1,0:T(8,128)S(1)}, f32[1,2,1,448,384]{4,3,2,1,0:T(8,128)S(1)}, u32[]{:S(2)}, u32[]{:S(2)}) collective-permute-start(f32[1,2,1,448,384]{4,3,2,1,0:T(8,128)S(1)} %get-tuple-element.24), channel_id=1, source_target_pairs={{0,1},{1,0},{2,3},{3,2},{4,5},{5,4},{6,7},{7,6},{8,9},{9,8},{10,11... | collective-permute-start | bytes 4128776 | tf_op jit(solution)/shard_map/ppermute | solution.py:147
  278.1 99.2 %collective-permute-start.22 = (f32[3,1,2,448,384]{4,3,2,1,0:T(8,128)}, f32[3,1,2,448,384]{4,3,2,1,0:T(8,128)}, u32[]{:S(2)}, u32[]{:S(2)}) collective-permute-start(f32[3,1,2,448,384]{4,3,2,1,0:T(8,128)} %slice.166), channel_id=1, source_target_pairs={{0,2},{1,3},{2,0},{3,1},{4,6},{5,7},{6,4},{7,5},{8,10},{9,11},{10,... | collective-permute-start | bytes 12386312 | tf_op jit(solution)/shard_map/ppermute | solution.py:147
  294.2 89.3 %collective-permute-start.23 = (f32[3,2,1,448,384]{4,3,2,1,0:T(8,128)}, f32[3,2,1,448,384]{4,3,2,1,0:T(8,128)}, u32[]{:S(2)}, u32[]{:S(2)}) collective-permute-start(f32[3,2,1,448,384]{4,3,2,1,0:T(8,128)} %slice.167), channel_id=1, source_target_pairs={{0,1},{1,0},{2,3},{3,2},{4,5},{5,4},{6,7},{7,6},{8,9},{9,8},{10,11... | collective-permute-start | bytes 12386312 | tf_op jit(solution)/shard_map/ppermute | solution.py:147
  305.9 82.1 %collective-permute-start.20 = (f32[896,896]{1,0:T(8,128)}, f32[896,896]{1,0:T(8,128)}, u32[]{:S(2)}, u32[]{:S(2)}) collective-permute-start(f32[896,896]{1,0:T(8,128)} %bitcast.7), channel_id=1, source_target_pairs={{0,16},{16,0},{1,17},{17,1},{2,18},{18,2},{3,19},{19,3},{4,20},{20... | collective-permute-start | bytes 9633800 | tf_op jit(solution)/shard_map/ppermute | solution.py:236
  306.0 160.2 %collective-permute-start.21 = (f32[448,896]{1,0:T(8,128)S(1)}, f32[448,896]{1,0:T(8,128)S(1)}, u32[]{:S(2)}, u32[]{:S(2)}) collective-permute-start(f32[448,896]{1,0:T(8,128)S(1)} %broadcast_multiply_fusion), channel_id=1, source_target_pairs={{0,16},{16,0},{1,17},{17,1},{2,18},{18,2},{3,19},{19,3},{4,20},{20... | collective-permute-start | bytes 4816904 | tf_op jit(solution)/shard_map/ppermute | solution.py:236
  466.3 8.0 copy-start
  480.2 27.5 %copy-start.3 = (bf16[1,448,2048]{2,1,0:T(8,128)(2,1)S(1)}, bf16[1,448,2048]{2,1,0:T(8,128)(2,1)}, u32[]{:S(2)}) copy-start(bf16[1,448,2048]{2,1,0:T(8,128)(2,1)} %param.3) | copy-start | bytes 5505028
  507.8 409.3 %collective-permute-start.24 = (f32[448,7168]{1,0:T(8,128)}, f32[448,7168]{1,0:T(8,128)}, u32[]{:S(2)}, u32[]{:S(2)}) collective-permute-start(f32[448,7168]{1,0:T(8,128)} %fusion.2), channel_id=1, source_target_pairs={{0,16},{16,0},{1,17},{17,1},{2,18},{18,2},{3,19},{19,3},{4,20},{20... | collective-permute-start | bytes 38535176 | tf_op jit(solution)/shard_map/ppermute | solution.py:236
  507.8 13.0 %collective-permute-start.41 = (bf16[1,1,1,448,512]{4,3,2,1,0:T(8,128)(2,1)S(1)}, bf16[1,1,1,448,512]{4,3,2,1,0:T(8,128)(2,1)S(1)}, u32[]{:S(2)}, u32[]{:S(2)}) collective-permute-start(bf16[1,1,1,448,512]{4,3,2,1,0:T(8,128)(2,1)S(1)} %slice_bitcast_fusion.2), channel_id=1, source_target_pairs={{0,1},{1,0},{2,3},{3,2},{4,5},{5,4},{6,7},{7,6},{8,9},{9,8},{10,11... | collective-permute-start | bytes 1376264 | tf_op jit(solution)/shard_map/ppermute | solution.py:147
  521.6 22.2 %collective-permute-start.42 = (bf16[1,1,2,448,512]{4,3,2,1,0:T(8,128)(2,1)}, bf16[1,1,2,448,512]{4,3,2,1,0:T(8,128)(2,1)}, u32[]{:S(2)}, u32[]{:S(2)}) collective-permute-start(bf16[1,1,2,448,512]{4,3,2,1,0:T(8,128)(2,1)} %constant_dynamic-update-slice_fusion.7), channel_id=1, source_target_pairs={{0,2},{1,3},{2,0},{3,1},{4,6},{5,7},{6,4},{7,5},{8,10},{9,11},{10,... | collective-permute-start | bytes 2752520 | tf_op jit(solution)/shard_map/ppermute | solution.py:147
  525.7 35.3 %collective-permute-start.25 = (bf16[1,1,1,448,1536]{4,3,2,1,0:T(8,128)(2,1)}, bf16[1,1,1,448,1536]{4,3,2,1,0:T(8,128)(2,1)S(1)}, u32[]{:S(2)}, u32[]{:S(2)}) collective-permute-start(bf16[1,1,1,448,1536]{4,3,2,1,0:T(8,128)(2,1)} %slice_bitcast_fusion.1), channel_id=1, source_target_pairs={{0,4},{1,5},{2,6},{3,7},{4,8},{5,9},{6,10},{7,11},{8,12},{9,13},{1... | collective-permute-start | bytes 4128776 | tf_op jit(solution)/shard_map/ppermute | solution.py:147
  546.0 54.2 %collective-permute-start.43 = (bf16[1,2,2,448,512]{4,3,2,1,0:T(8,128)(2,1)}, bf16[1,2,2,448,512]{4,3,2,1,0:T(8,128)(2,1)}, u32[]{:S(2)}, u32[]{:S(2)}) collective-permute-start(bf16[1,2,2,448,512]{4,3,2,1,0:T(8,128)(2,1)} %constant_dynamic-update-slice_fusion.5), channel_id=1, source_target_pairs={{0,4},{1,5},{2,6},{3,7},{4,8},{5,9},{6,10},{7,11},{8,12},{9,13},{1... | collective-permute-start | bytes 5505032 | tf_op jit(solution)/shard_map/ppermute | solution.py:147
  546.0 82.2 %collective-permute-start.26 = (bf16[1,1,1,448,1536]{4,3,2,1,0:T(8,128)(2,1)}, bf16[1,1,1,448,1536]{4,3,2,1,0:T(8,128)(2,1)}, u32[]{:S(2)}, u32[]{:S(2)}) collective-permute-start(bf16[1,1,1,448,1536]{4,3,2,1,0:T(8,128)(2,1)} %slice_bitcast_fusion.1), channel_id=1, source_target_pairs={{0,12},{1,13},{2,14},{3,15},{4,0},{5,1},{6,2},{7,3},{8,4},{9,5},{1... | collective-permute-start | bytes 4128776 | tf_op jit(solution)/shard_map/ppermute | solution.py:147
  549.8 174.8 %collective-permute-start.44 = (bf16[1,2,2,448,512]{4,3,2,1,0:T(8,128)(2,1)}, bf16[1,2,2,448,512]{4,3,2,1,0:T(8,128)(2,1)S(1)}, u32[]{:S(2)}, u32[]{:S(2)}) collective-permute-start(bf16[1,2,2,448,512]{4,3,2,1,0:T(8,128)(2,1)} %constant_dynamic-update-slice_fusion.5), channel_id=1, source_target_pairs={{0,12},{1,13},{2,14},{3,15},{4,0},{5,1},{6,2},{7,3},{8,4},{9,5},{1... | collective-permute-start | bytes 5505032 | tf_op jit(solution)/shard_map/ppermute | solution.py:147
  561.0 122.8 %collective-permute-start.27 = (bf16[1,1,1,224,1536]{4,3,2,1,0:T(8,128)(2,1)S(1)}, bf16[1,1,1,224,1536]{4,3,2,1,0:T(8,128)(2,1)S(1)}, u32[]{:S(2)}, u32[]{:S(2)}) collective-permute-start(bf16[1,1,1,224,1536]{4,3,2,1,0:T(8,128)(2,1)S(1)} %slice.168), channel_id=1, source_target_pairs={{0,4},{1,5},{2,6},{3,7},{4,8},{5,9},{6,10},{7,11},{8,12},{9,13},{1... | collective-permute-start | bytes 2064392 | tf_op jit(solution)/shard_map/ppermute | solution.py:147
  601.5 124.7 %collective-permute-start.45 = (bf16[1,1,2,448,512]{4,3,2,1,0:T(8,128)(2,1)S(1)}, bf16[1,1,2,448,512]{4,3,2,1,0:T(8,128)(2,1)S(1)}, u32[]{:S(2)}, u32[]{:S(2)}) collective-permute-start(bf16[1,1,2,448,512]{4,3,2,1,0:T(8,128)(2,1)S(1)} %slice.183), channel_id=1, source_target_pairs={{0,4},{1,5},{2,6},{3,7},{4,8},{5,9},{6,10},{7,11},{8,12},{9,13},{1... | collective-permute-start | bytes 2752520 | tf_op jit(solution)/shard_map/ppermute | solution.py:147
  629.4 87.1 %collective-permute-start.28 = (bf16[1,1,1,224,1536]{4,3,2,1,0:T(8,128)(2,1)S(1)}, bf16[1,1,1,224,1536]{4,3,2,1,0:T(8,128)(2,1)S(1)}, u32[]{:S(2)}, u32[]{:S(2)}) collective-permute-start(bf16[1,1,1,224,1536]{4,3,2,1,0:T(8,128)(2,1)S(1)} %slice.169), channel_id=1, source_target_pairs={{0,12},{1,13},{2,14},{3,15},{4,0},{5,1},{6,2},{7,3},{8,4},{9,5},{1... | collective-permute-start | bytes 2064392 | tf_op jit(solution)/shard_map/ppermute | solution.py:147
  722.6 33.1 %collective-permute-start.38 = (bf16[4,1,1,448,384]{4,3,2,1,0:T(8,128)(2,1)S(1)}, bf16[4,1,1,448,384]{4,3,2,1,0:T(8,128)(2,1)S(1)}, u32[]{:S(2)}, u32[]{:S(2)}) collective-permute-start(bf16[4,1,1,448,384]{4,3,2,1,0:T(8,128)(2,1)S(1)} %get-tuple-element.15), channel_id=1, source_target_pairs={{0,2},{1,3},{2,0},{3,1},{4,6},{5,7},{6,4},{7,5},{8,10},{9,11},{10,... | collective-permute-start | bytes 4128776 | tf_op jit(solution)/shard_map/ppermute | solution.py:147
  724.0 60.2 %collective-permute-start.35 = (bf16[4,1,1,448,384]{4,3,2,1,0:T(8,128)(2,1)S(1)}, bf16[4,1,1,448,384]{4,3,2,1,0:T(8,128)(2,1)S(1)}, u32[]{:S(2)}, u32[]{:S(2)}) collective-permute-start(bf16[4,1,1,448,384]{4,3,2,1,0:T(8,128)(2,1)S(1)} %get-tuple-element.20), channel_id=1, source_target_pairs={{0,2},{1,3},{2,0},{3,1},{4,6},{5,7},{6,4},{7,5},{8,10},{9,11},{10,... | collective-permute-start | bytes 4128776 | tf_op jit(solution)/shard_map/ppermute | solution.py:147
  724.6 66.7 %copy-start.8 = (bf16[1,2,2,448,512]{4,3,2,1,0:T(8,128)(2,1)}, bf16[1,2,2,448,512]{4,3,2,1,0:T(8,128)(2,1)S(1)}, u32[]{:S(2)}) copy-start(bf16[1,2,2,448,512]{4,3,2,1,0:T(8,128)(2,1)S(1)} %collective-permute-done.44) | copy-start | bytes 5505028
  724.6 62.3 %collective-permute-start.32 = (bf16[4,1,1,448,384]{4,3,2,1,0:T(8,128)(2,1)S(1)}, bf16[4,1,1,448,384]{4,3,2,1,0:T(8,128)(2,1)S(1)}, u32[]{:S(2)}, u32[]{:S(2)}) collective-permute-start(bf16[4,1,1,448,384]{4,3,2,1,0:T(8,128)(2,1)S(1)} %get-tuple-element.21), channel_id=1, source_target_pairs={{0,1},{1,0},{2,3},{3,2},{4,5},{5,4},{6,7},{7,6},{8,9},{9,8},{10,11... | collective-permute-start | bytes 4128776 | tf_op jit(solution)/shard_map/ppermute | solution.py:147
  726.1 65.2 %copy-start.11 = (bf16[1,1,2,448,512]{4,3,2,1,0:T(8,128)(2,1)}, bf16[1,1,2,448,512]{4,3,2,1,0:T(8,128)(2,1)S(1)}, u32[]{:S(2)}) copy-start(bf16[1,1,2,448,512]{4,3,2,1,0:T(8,128)(2,1)S(1)} %collective-permute-done.45) | copy-start | bytes 2752516
  726.1 62.6 %collective-permute-start.29 = (bf16[4,1,1,448,384]{4,3,2,1,0:T(8,128)(2,1)S(1)}, bf16[4,1,1,448,384]{4,3,2,1,0:T(8,128)(2,1)S(1)}, u32[]{:S(2)}, u32[]{:S(2)}) collective-permute-start(bf16[4,1,1,448,384]{4,3,2,1,0:T(8,128)(2,1)S(1)} %get-tuple-element.22), channel_id=1, source_target_pairs={{0,1},{1,0},{2,3},{3,2},{4,5},{5,4},{6,7},{7,6},{8,9},{9,8},{10,11... | collective-permute-start | bytes 4128776 | tf_op jit(solution)/shard_map/ppermute | solution.py:147
  755.7 35.7 %collective-permute-start.46 = (bf16[1,1,2,448,512]{4,3,2,1,0:T(8,128)(2,1)S(1)}, bf16[1,1,2,448,512]{4,3,2,1,0:T(8,128)(2,1)S(1)}, u32[]{:S(2)}, u32[]{:S(2)}) collective-permute-start(bf16[1,1,2,448,512]{4,3,2,1,0:T(8,128)(2,1)S(1)} %slice.184), channel_id=1, source_target_pairs={{0,12},{1,13},{2,14},{3,15},{4,0},{5,1},{6,2},{7,3},{8,4},{9,5},{1... | collective-permute-start | bytes 2752520 | tf_op jit(solution)/shard_map/ppermute | solution.py:147
  784.2 62.9 %collective-permute-start.39 = (bf16[4,2,1,448,384]{4,3,2,1,0:T(8,128)(2,1)}, bf16[4,2,1,448,384]{4,3,2,1,0:T(8,128)(2,1)}, u32[]{:S(2)}, u32[]{:S(2)}) collective-permute-start(bf16[4,2,1,448,384]{4,3,2,1,0:T(8,128)(2,1)} %constant_dynamic-update-slice_fusion.11), channel_id=1, source_target_pairs={{0,1},{1,0},{2,3},{3,2},{4,5},{5,4},{6,7},{7,6},{8,9},{9,8},{10,11... | collective-permute-start | bytes 8257544 | tf_op jit(solution)/shard_map/ppermute | solution.py:147
  787.0 117.3 %collective-permute-start.36 = (bf16[4,2,1,448,384]{4,3,2,1,0:T(8,128)(2,1)}, bf16[4,2,1,448,384]{4,3,2,1,0:T(8,128)(2,1)}, u32[]{:S(2)}, u32[]{:S(2)}) collective-permute-start(bf16[4,2,1,448,384]{4,3,2,1,0:T(8,128)(2,1)} %constant_dynamic-update-slice_fusion.15), channel_id=1, source_target_pairs={{0,1},{1,0},{2,3},{3,2},{4,5},{5,4},{6,7},{7,6},{8,9},{9,8},{10,11... | collective-permute-start | bytes 8257544 | tf_op jit(solution)/shard_map/ppermute | solution.py:147
  788.8 117.8 %collective-permute-start.33 = (bf16[4,1,2,448,384]{4,3,2,1,0:T(8,128)(2,1)}, bf16[4,1,2,448,384]{4,3,2,1,0:T(8,128)(2,1)}, u32[]{:S(2)}, u32[]{:S(2)}) collective-permute-start(bf16[4,1,2,448,384]{4,3,2,1,0:T(8,128)(2,1)} %constant_dynamic-update-slice_fusion.19), channel_id=1, source_target_pairs={{0,2},{1,3},{2,0},{3,1},{4,6},{5,7},{6,4},{7,5},{8,10},{9,11},{10,... | collective-permute-start | bytes 8257544 | tf_op jit(solution)/shard_map/ppermute | solution.py:147
  792.3 121.0 %collective-permute-start.30 = (bf16[4,1,2,448,384]{4,3,2,1,0:T(8,128)(2,1)}, bf16[4,1,2,448,384]{4,3,2,1,0:T(8,128)(2,1)}, u32[]{:S(2)}, u32[]{:S(2)}) collective-permute-start(bf16[4,1,2,448,384]{4,3,2,1,0:T(8,128)(2,1)} %constant_dynamic-update-slice_fusion.23), channel_id=1, source_target_pairs={{0,2},{1,3},{2,0},{3,1},{4,6},{5,7},{6,4},{7,5},{8,10},{9,11},{10,... | collective-permute-start | bytes 8257544 | tf_op jit(solution)/shard_map/ppermute | solution.py:147
  795.9 10.6 %slice-start.6 = ((s8[5505024]{0:T(1024)(128)(4,1)}), s8[4194304]{0:T(1024)(128)(4,1)S(1)}, s32[]{:S(2)}) async-start(s8[5505024]{0:T(1024)(128)(4,1)} %bitcast.56), calls=%async_computation.6 | async-start | bytes 8388608
  801.3 7.7 slice-start.4
  806.5 40.6 %slice-start.8 = ((s8[5505024]{0:T(1024)(128)(4,1)}), s8[4194304]{0:T(1024)(128)(4,1)S(1)}, s32[]{:S(2)}) async-start(s8[5505024]{0:T(1024)(128)(4,1)} %bitcast.59), calls=%async_computation.8 | async-start | bytes 8388608
  809.0 38.1 %slice-start.9 = ((s8[5505024]{0:T(1024)(128)(4,1)}), s8[1310720]{0:T(1024)(128)(4,1)S(1)}, s32[]{:S(2)}) async-start(s8[5505024]{0:T(1024)(128)(4,1)} %bitcast.59), calls=%async_computation.9 | async-start | bytes 2621440
  849.4 61.5 %copy-start.7 = (bf16[4,2,2,448,384]{4,3,2,1,0:T(8,128)(2,1)}, bf16[4,2,2,448,384]{4,3,2,1,0:T(8,128)(2,1)S(1)}, u32[]{:S(2)}) copy-start(bf16[4,2,2,448,384]{4,3,2,1,0:T(8,128)(2,1)S(1)} %constant_dynamic-update-slice_fusion.9) | copy-start | bytes 16515076
  906.6 10.4 %copy-start.6 = (bf16[4,2,2,448,384]{4,3,2,1,0:T(8,128)(2,1)}, bf16[4,2,2,448,384]{4,3,2,1,0:T(8,128)(2,1)S(1)}, u32[]{:S(2)}) copy-start(bf16[4,2,2,448,384]{4,3,2,1,0:T(8,128)(2,1)S(1)} %constant_dynamic-update-slice_fusion.13) | copy-start | bytes 16515076
  913.3 23.1 %slice-start = ((s8[7340032]{0:T(1024)(128)(4,1)}), s8[4194304]{0:T(1024)(128)(4,1)S(1)}, s32[]{:S(2)}) async-start(s8[7340032]{0:T(1024)(128)(4,1)} %bitcast.44), calls=%async_computation | async-start | bytes 8388608
  917.0 19.3 %slice-start.1 = ((s8[7340032]{0:T(1024)(128)(4,1)}), s8[3145728]{0:T(1024)(128)(4,1)S(1)}, s32[]{:S(2)}) async-start(s8[7340032]{0:T(1024)(128)(4,1)} %bitcast.44), calls=%async_computation.1 | async-start | bytes 6291456
  946.2 11.9 %slice-start.2 = ((s8[6422528]{0:T(1024)(128)(4,1)}), s8[4194304]{0:T(1024)(128)(4,1)S(1)}, s32[]{:S(2)}) async-start(s8[6422528]{0:T(1024)(128)(4,1)} %bitcast.51), calls=%async_computation.2 | async-start | bytes 8388608
  946.4 47.4 %collective-permute-start.47 = (f32[448,512]{1,0:T(8,128)S(1)}, f32[448,512]{1,0:T(8,128)S(1)}, u32[]{:S(2)}, u32[]{:S(2)}) collective-permute-start(f32[448,512]{1,0:T(8,128)S(1)} %slice_add_fusion), channel_id=1, source_target_pairs={{0,16},{16,0},{1,17},{17,1},{2,18},{18,2},{3,19},{19,3},{4,20},{20... | collective-permute-start | bytes 2752520 | tf_op jit(solution)/shard_map/ppermute | solution.py:236
  946.5 11.6 %slice-start.3 = ((s8[6422528]{0:T(1024)(128)(4,1)}), s8[2228224]{0:T(1024)(128)(4,1)S(1)}, s32[]{:S(2)}) async-start(s8[6422528]{0:T(1024)(128)(4,1)} %bitcast.51), calls=%async_computation.3 | async-start | bytes 4456448
  988.5 2.3 collective-permute-start.31
  989.1 2.7 collective-permute-start.34
  989.3 3.5 collective-permute-start.37
  989.9 3.9 collective-permute-start.40
  (10 other events, 38.4 us)

commit v3 on v2

--- a/solution.py
+++ b/solution.py
@@ -285,7 +285,7 @@
     panels = fill(panels, moved(behind[1], 1), size0)
     panels = panels.reshape(width, panel)
 
-    width0, width1, _ = widths_of(columns)
+    width0, width1, width2 = widths_of(columns)
     fork = width0 + width1
     w_late = gather_along(spread(weights[:, fork:]), torus, 2)
     weights = after(weights, early[:1, :1, :1, :8, :128])
@@ -296,11 +296,23 @@
     for turn, (size, dim) in enumerate(((half0, 2), (half1, 1), (width0 - half0, 2), (width1 - half1, 1))):
         first = (0, width0, half0, width0 + half1)[turn]
         w_mids.append(gather_along(w_early[..., first : first + size], torus, dim))
-    gathered_weights = [gather_along(w_late, torus, 0)] + [
-        gather_along(mid, torus, 1 if turn % 2 == 0 else 2)
-        for turn, mid in enumerate(w_mids)
-    ]
-    gathered_weights = [w.reshape(width, -1) for w in gathered_weights]
+    ends = (1, 2, 1, 2)
+    sizes = (half0, half1, width0 - half0, width1 - half1)
+    early_columns = width2 + sizes[0] + sizes[1]
+    halves = (
+        blank(torus + (rows, early_columns), weights.dtype),
+        blank(torus + (rows, sizes[2] + sizes[3]), weights.dtype),
+    )
+    lanes = (width2, width2 + sizes[0], 0, sizes[2])
+    pieces = [[(mid, {dim: along(torus, dim)})] for mid, dim in zip(w_mids, ends)]
+    first = fill(halves[0], [(w_late, {0: along(torus, 0)})])
+    first = fill(fill(first, pieces[0], lanes[0]), pieces[1], lanes[1])
+    first = fill(first, arrivals(w_late, torus, 0))
+    second = fill(fill(halves[1], pieces[2], lanes[2]), pieces[3], lanes[3])
+    received = [arrivals(mid, torus, dim) for mid, dim in zip(w_mids, ends)]
+    first = fill(fill(first, received[0], lanes[0]), received[1], lanes[1])
+    second = fill(fill(second, received[2], lanes[2]), received[3], lanes[3])
+    gathered_weights = [w.reshape(width, -1) for w in (first, second)]
 
     corner = scaling * plane.reshape(-1, panel)[:panel]
     corner = corner + swapped(corner)
@@ -324,7 +336,14 @@
         part = jnp.dot(both, weight, preferred_element_type=jnp.float32)
         part = part[:rows] + part[rows:]
         solved.append(part + swapped(part))
-    return (reduced_gram, jnp.concatenate([solved[i] for i in (1, 3, 2, 4, 0)], axis=1))
+    columns_of = [
+        solved[0][:, lanes[0] : lanes[1]],
+        solved[1][:, : lanes[3]],
+        solved[0][:, lanes[1] :],
+        solved[1][:, lanes[3] :],
+        solved[0][:, :width2],
+    ]
+    return (reduced_gram, jnp.concatenate(columns_of, axis=1))
 
 
 def solution(mesh):

time: 1000 us -> 991 us (level)
  matrix products: 93.1 us -> 80.4 us
  waiting for transfers between devices: 607 us -> 596 us
    dot_general x5 -> x2, matrix products: 51.7 us -> 39 us  [per_device(): part = jnp.dot(both, weight, preferred_element_type=jnp.float32)]
  transfers between devices with their start and end apart: 48 -> 45, of which waited for: 31 -> 29; matrix products, arithmetic and copies ran while one was open for 18% -> 16% of each run, Pallas kernels for 7% -> 7%
where the time goes in v3:
time: 991 us; the launch traced here: 983 us
  waiting for transfers between devices  596 us (60%)
  local copies, waits for them, and re-layouts  147 us (15%)
  matrix products  80.4 us (8%)
  Pallas kernels  71.4 us (7%)
  starting transfers between devices  52 us (5%)
  other arithmetic  34.5 us (3%)
    ppermute x34, waiting for transfers between devices, shifted(): return lax.ppermute(value, 'row', pairs)  545 us
    dynamic_update_slice x52, local copies, waits for them, and re-layouts, fill(): lax.dynamic_update_slice(buffer, chunk, tuple((jnp.asarray(i, jnp.int32)...  107 us
    pallas_call x2, Pallas kernels, eliminate(): pl.pallas_call(functools.partial(factor_body, blocks), out_shape=(whole,...  71.3 us
    ppermute x6, waiting for transfers between devices, torus_sum(): total = total + lax.ppermute(value, 'row', pairs)  47.5 us
    ppermute x34, starting transfers between devices, shifted(): return lax.ppermute(value, 'row', pairs)  42.6 us
    dot_general x3, matrix products, dot(): lax.dot_general(a, b, (dims, ((), ())), precision=precision, preferred_el...  41.5 us
    dot_general x2, matrix products, per_device(): part = jnp.dot(both, weight, preferred_element_type=jnp.float32)  39 us
    convert_element_type x1, other arithmetic, per_device(): both = jnp.concatenate([high.astype(jnp.bfloat16), rest], axis=0)  20.3 us
  transfers between devices with their start and end apart: 45, of which 29 were waited for; matrix products, arithmetic and copies ran while one was open for 16% of the time, Pallas kernels for 7%

profile of v3, /device:TPU:0, one launch (start us, length us, event | category | flops | bytes accessed | tf_op | source)
XLA Modules:
  0.0 983.0 jit_solution(7101805086170263075)
XLA Ops:
  3.5 3.1 collective-permute-start.6
  8.6 31.3 %collective-permute-done.6 = f32[1,1,1,448,768]{4,3,2,1,0:T(8,128)S(1)} collective-permute-done((f32[1,1,1,448,768]{4,3,2,1,0:T(8,128)}, f32[1,1,1,448,768]{4,3,2,1,0:T(8,128)S(1)}, u32[]{:S(2)}, u32[]{:S(2)}) %collective-permute-start.6) | collective-permute-done | bytes 1376288 | tf_op jit(solution)/shard_map/ppermute | solution.py:147
  40.8 27.5 %collective-permute-done.7 = f32[1,1,1,448,768]{4,3,2,1,0:T(8,128)} collective-permute-done((f32[1,1,1,448,768]{4,3,2,1,0:T(8,128)}, f32[1,1,1,448,768]{4,3,2,1,0:T(8,128)}, u32[]{:S(2)}, u32[]{:S(2)}) %collective-permute-start.7) | collective-permute-done | bytes 1376288 | tf_op jit(solution)/shard_map/ppermute | solution.py:147
  69.4 3.1 collective-permute-start.9
  74.8 2.5 constant_dynamic-update-slice_fusion.56
  77.3 9.7 collective-permute-done.8
  89.0 9.0 collective-permute-done.9
  98.9 8.1 fusion.18
  111.4 62.3 %collective-permute-done.12 = f32[1,1,1,448,128]{4,3,2,1,0:T(8,128)S(1)} collective-permute-done((f32[1,1,1,448,128]{4,3,2,1,0:T(8,128)S(1)}, f32[1,1,1,448,128]{4,3,2,1,0:T(8,128)S(1)}, u32[]{:S(2)}, u32[]{:S(2)}) %collective-permute-start.12) | collective-permute-done | bytes 229408 | tf_op jit(solution)/shard_map/ppermute | solution.py:147
  177.8 8.3 collective-permute-done.13
  187.6 3.3 collective-permute-start.15
  190.8 2.4 fusion.11
  194.0 33.9 %collective-permute-done.2 = f32[8,128]{1,0:T(8,128)S(1)} collective-permute-done((f32[8,128]{1,0:T(8,128)S(1)}, f32[8,128]{1,0:T(8,128)S(1)}, u32[]{:S(2)}, u32[]{:S(2)}) %collective-permute-start.2) | collective-permute-done | bytes 4128 | tf_op jit(solution)/shard_map/ppermute | solution.py:227
  230.0 2.4 collective-permute-done.1
  232.7 5.1 collective-permute-done
  238.4 2.6 collective-permute-start.5
  253.6 3.9 collective-permute-start.17
  258.5 2.3 constant_dynamic-update-slice_fusion.41
  260.8 3.6 constant_dynamic-update-slice_fusion.52
  267.6 3.7 constant_dynamic-update-slice_fusion.49
  274.6 4.4 slice.162
  279.3 5.5 constant_dynamic-update-slice_fusion.36
  284.8 5.4 constant_dynamic-update-slice_fusion.35
  290.3 4.5 slice.163
  295.2 2.3 constant_dynamic-update-slice_fusion.34
  300.4 4.0 collective-permute-done.19
  308.2 70.8 %collective-permute-done.22 = f32[3,1,2,448,384]{4,3,2,1,0:T(8,128)} collective-permute-done((f32[3,1,2,448,384]{4,3,2,1,0:T(8,128)}, f32[3,1,2,448,384]{4,3,2,1,0:T(8,128)}, u32[]{:S(2)}, u32[]{:S(2)}) %collective-permute-start.22) | collective-permute-done | bytes 4128800 | tf_op jit(solution)/shard_map/ppermute | solution.py:147
  379.0 4.5 constant_dynamic-update-slice_fusion.31
  383.5 2.2 collective-permute-done.23
  385.7 4.5 constant_dynamic-update-slice_fusion.30
  390.2 4.9 bitcast_add_fusion.a_ref
  396.9 34.0 %shard_map.48 = (f32[896,896]{1,0:T(8,128)}, f32[896,896]{1,0:T(8,128)}) custom-call(f32[896,896]{1,0:T(8,128)} %bitcast_add_fusion.a_ref, f32[896,896]{1,0:T(8,128)} %broadcast_in_dim.14.done_ref), custom_call_target="tpu_custom_call" | custom-call | flops 20000000000 | bytes 12845056 | tf_op jit(solution)/shard_map/pallas_call | solution.py:107
  430.9 37.4 %shard_map.49 = (f32[896,896]{1,0:T(8,128)}, f32[896,896]{1,0:T(8,128)}) custom-call(f32[896,896]{1,0:T(8,128)} %get-tuple-element.7.a_ref, f32[896,896]{1,0:T(8,128)} %get-tuple-element.8.done_ref), custom_call_target="tpu_custom_call" | custom-call | flops 20000000000 | bytes 12845056 | tf_op jit(solution)/shard_map/pallas_call | solution.py:107
  468.3 8.0 fusion.8
  476.3 5.9 fusion.19
  482.3 27.5 %fusion.2 = f32[448,7168]{1,0:T(8,128)} fusion(f32[7168,896]{1,0:T(8,128)} %bitcast.8, s32[448]{0:T(512)S(1)} %iota_add_fusion, f32[]{:T(128)} %bitcast.2, f32[448,896]{1,0:T(8,128)S(1)} %fusion.19, f32[896,896]{1,0:T(8,128)S(1)} %copy-done, s32[]{:T(128)S(6)} %select_n.305, f32[]{:T(128)} %bitcast.4, pred[]{:T(512)} %lt.205, f32[1,448,7168]{2,1,0:T(8,128)} %param.2), kind=kOutput, calls=%fused_computation.5 | convolution fusion | flops 17281015808 | bytes 54593548 | tf_op jit(solution)/shard_map/dot_general | solution.py:21
  512.3 10.5 %collective-permute-done.25 = bf16[1,1,1,448,512]{4,3,2,1,0:T(8,128)(2,1)S(1)} collective-permute-done((bf16[1,1,1,448,512]{4,3,2,1,0:T(8,128)(2,1)S(1)}, bf16[1,1,1,448,512]{4,3,2,1,0:T(8,128)(2,1)S(1)}, u32[]{:S(2)}, u32[]{:S(2)}) %collective-permute-start.25) | collective-permute-done | bytes 458784 | tf_op jit(solution)/shard_map/ppermute | solution.py:147
  523.9 2.2 constant_dynamic-update-slice_fusion.27
  527.3 18.5 %collective-permute-done.26 = bf16[1,1,2,448,512]{4,3,2,1,0:T(8,128)(2,1)} collective-permute-done((bf16[1,1,2,448,512]{4,3,2,1,0:T(8,128)(2,1)}, bf16[1,1,2,448,512]{4,3,2,1,0:T(8,128)(2,1)}, u32[]{:S(2)}, u32[]{:S(2)}) %collective-permute-start.26) | collective-permute-done | bytes 917536 | tf_op jit(solution)/shard_map/ppermute | solution.py:147
  548.0 3.8 collective-permute-start.28
  551.9 10.6 %collective-permute-done.27 = bf16[1,1,1,448,1536]{4,3,2,1,0:T(8,128)(2,1)S(1)} collective-permute-done((bf16[1,1,1,448,1536]{4,3,2,1,0:T(8,128)(2,1)}, bf16[1,1,1,448,1536]{4,3,2,1,0:T(8,128)(2,1)S(1)}, u32[]{:S(2)}, u32[]{:S(2)}) %collective-permute-start.27) | collective-permute-done | bytes 1376288 | tf_op jit(solution)/shard_map/ppermute | solution.py:147
  563.9 38.0 %collective-permute-done.33 = bf16[1,2,2,448,512]{4,3,2,1,0:T(8,128)(2,1)} collective-permute-done((bf16[1,2,2,448,512]{4,3,2,1,0:T(8,128)(2,1)}, bf16[1,2,2,448,512]{4,3,2,1,0:T(8,128)(2,1)}, u32[]{:S(2)}, u32[]{:S(2)}) %collective-permute-start.33) | collective-permute-done | bytes 1835040 | tf_op jit(solution)/shard_map/ppermute | solution.py:147
  603.2 26.7 %collective-permute-done.28 = bf16[1,1,1,448,1536]{4,3,2,1,0:T(8,128)(2,1)} collective-permute-done((bf16[1,1,1,448,1536]{4,3,2,1,0:T(8,128)(2,1)}, bf16[1,1,1,448,1536]{4,3,2,1,0:T(8,128)(2,1)}, u32[]{:S(2)}, u32[]{:S(2)}) %collective-permute-start.28) | collective-permute-done | bytes 1376288 | tf_op jit(solution)/shard_map/ppermute | solution.py:147
  633.8 2.5 constant_dynamic-update-slice_fusion.22
  636.3 49.1 %collective-permute-done.29 = bf16[1,1,1,224,1536]{4,3,2,1,0:T(8,128)(2,1)S(1)} collective-permute-done((bf16[1,1,1,224,1536]{4,3,2,1,0:T(8,128)(2,1)S(1)}, bf16[1,1,1,224,1536]{4,3,2,1,0:T(8,128)(2,1)S(1)}, u32[]{:S(2)}, u32[]{:S(2)}) %collective-permute-start.29) | collective-permute-done | bytes 688160 | tf_op jit(solution)/shard_map/ppermute | solution.py:147
  686.3 31.8 %collective-permute-done.30 = bf16[1,1,1,224,1536]{4,3,2,1,0:T(8,128)(2,1)S(1)} collective-permute-done((bf16[1,1,1,224,1536]{4,3,2,1,0:T(8,128)(2,1)S(1)}, bf16[1,1,1,224,1536]{4,3,2,1,0:T(8,128)(2,1)S(1)}, u32[]{:S(2)}, u32[]{:S(2)}) %collective-permute-start.30) | collective-permute-done | bytes 688160 | tf_op jit(solution)/shard_map/ppermute | solution.py:147
  719.0 5.2 fusion.17
  728.4 28.9 %collective-permute-done.31 = bf16[4,1,1,448,384]{4,3,2,1,0:T(8,128)(2,1)S(1)} collective-permute-done((bf16[4,1,1,448,384]{4,3,2,1,0:T(8,128)(2,1)S(1)}, bf16[4,1,1,448,384]{4,3,2,1,0:T(8,128)(2,1)S(1)}, u32[]{:S(2)}, u32[]{:S(2)}) %collective-permute-start.31) | collective-permute-done | bytes 1376288 | tf_op jit(solution)/shard_map/ppermute | solution.py:147
  761.9 23.9 %collective-permute-done.40 = bf16[4,1,1,448,384]{4,3,2,1,0:T(8,128)(2,1)S(1)} collective-permute-done((bf16[4,1,1,448,384]{4,3,2,1,0:T(8,128)(2,1)S(1)}, bf16[4,1,1,448,384]{4,3,2,1,0:T(8,128)(2,1)S(1)}, u32[]{:S(2)}, u32[]{:S(2)}) %collective-permute-start.40) | collective-permute-done | bytes 1376288 | tf_op jit(solution)/shard_map/ppermute | solution.py:147
  796.0 3.7 constant_dynamic-update-slice_fusion.17
  799.7 3.9 constant_dynamic-update-slice_fusion.14
  803.6 3.0 constant_dynamic-update-slice_fusion.13
  810.1 3.6 constant_dynamic-update-slice_fusion.5
  813.7 3.7 constant_dynamic-update-slice_fusion.2
  817.4 30.1 %collective-permute-done.37 = bf16[4,1,2,448,384]{4,3,2,1,0:T(8,128)(2,1)} collective-permute-done((bf16[4,1,2,448,384]{4,3,2,1,0:T(8,128)(2,1)}, bf16[4,1,2,448,384]{4,3,2,1,0:T(8,128)(2,1)}, u32[]{:S(2)}, u32[]{:S(2)}) %collective-permute-start.37) | collective-permute-done | bytes 2752544 | tf_op jit(solution)/shard_map/ppermute | solution.py:147
  847.5 3.6 constant_dynamic-update-slice_fusion.9
  851.1 3.7 constant_dynamic-update-slice_fusion.8
  854.8 50.5 %collective-permute-done.42 = bf16[4,1,2,448,384]{4,3,2,1,0:T(8,128)(2,1)} collective-permute-done((bf16[4,1,2,448,384]{4,3,2,1,0:T(8,128)(2,1)}, bf16[4,1,2,448,384]{4,3,2,1,0:T(8,128)(2,1)}, u32[]{:S(2)}, u32[]{:S(2)}) %collective-permute-start.42) | collective-permute-done | bytes 2752544 | tf_op jit(solution)/shard_map/ppermute | solution.py:147
  905.3 3.7 constant_dynamic-update-slice_fusion.1
  909.0 3.9 constant_dynamic-update-slice_fusion
  913.0 20.3 %reduce-precision_convert_fusion = (bf16[448,7168]{1,0:T(8,128)(2,1)}, bf16[448,7168]{1,0:T(8,128)(2,1)}, f32[448,7168]{1,0:T(8,128)}) fusion(f32[448,7168]{1,0:T(8,128)} %fusion.2, f32[448,7168]{1,0:T(8,128)} %collective-permute-done.24), kind=kLoop, calls=%fused_computation.2 | loop fusion | flops 16056320 | bytes 51380224 | tf_op jit(solution)/shard_map/convert_element_type | solution.py:333
  933.3 21.6 %fusion.4 = f32[896,1280]{1,0:T(8,128)S(1)} fusion(bf16[7168,1280]{1,0:T(8,128)(2,1)S(1)} %bitcast.40, bf16[448,7168]{1,0:T(8,128)(2,1)} %get-tuple-element.13, bf16[448,7168]{1,0:T(8,128)(2,1)} %get-tuple-element.12), kind=kOutput, calls=%fused_computation.9 | convolution fusion | flops 16467361792 | bytes 35782656 | tf_op jit(solution)/shard_map/dot_general | solution.py:336
  958.7 17.4 %fusion.3 = f32[896,768]{1,0:T(8,128)S(1)} fusion(bf16[7168,768]{1,0:T(8,128)(2,1)} %bitcast.13, bf16[448,7168]{1,0:T(8,128)(2,1)} %get-tuple-element.13, bf16[448,7168]{1,0:T(8,128)(2,1)} %get-tuple-element.12), kind=kOutput, calls=%fused_computation.8 | convolution fusion | flops 9890693120 | bytes 26607616 | tf_op jit(solution)/shard_map/dot_general | solution.py:336
  976.8 2.8 collective-permute-done.44
  (181 shorter events, 100.0 us)
Async XLA Ops:
  3.5 36.4 %collective-permute-start.6 = (f32[1,1,1,448,768]{4,3,2,1,0:T(8,128)}, f32[1,1,1,448,768]{4,3,2,1,0:T(8,128)S(1)}, u32[]{:S(2)}, u32[]{:S(2)}) collective-permute-start(f32[1,1,1,448,768]{4,3,2,1,0:T(8,128)} %slice_bitcast_fusion), channel_id=1, source_target_pairs={{0,4},{1,5},{2,6},{3,7},{4,8},{5,9},{6,10},{7,11},{8,12},{9,13},{1... | collective-permute-start | bytes 4128776 | tf_op jit(solution)/shard_map/ppermute | solution.py:147
  6.6 61.7 %collective-permute-start.7 = (f32[1,1,1,448,768]{4,3,2,1,0:T(8,128)}, f32[1,1,1,448,768]{4,3,2,1,0:T(8,128)}, u32[]{:S(2)}, u32[]{:S(2)}) collective-permute-start(f32[1,1,1,448,768]{4,3,2,1,0:T(8,128)} %slice_bitcast_fusion), channel_id=1, source_target_pairs={{0,12},{1,13},{2,14},{3,15},{4,0},{5,1},{6,2},{7,3},{8,4},{9,5},{1... | collective-permute-start | bytes 4128776 | tf_op jit(solution)/shard_map/ppermute | solution.py:147
  40.8 46.3 %collective-permute-start.8 = (f32[1,1,1,224,768]{4,3,2,1,0:T(8,128)}, f32[1,1,1,224,768]{4,3,2,1,0:T(8,128)}, u32[]{:S(2)}, u32[]{:S(2)}) collective-permute-start(f32[1,1,1,224,768]{4,3,2,1,0:T(8,128)} %slice.150), channel_id=1, source_target_pairs={{0,4},{1,5},{2,6},{3,7},{4,8},{5,9},{6,10},{7,11},{8,12},{9,13},{1... | collective-permute-start | bytes 2064392 | tf_op jit(solution)/shard_map/ppermute | solution.py:147
  69.4 28.6 %collective-permute-start.9 = (f32[1,1,1,224,768]{4,3,2,1,0:T(8,128)S(1)}, f32[1,1,1,224,768]{4,3,2,1,0:T(8,128)S(1)}, u32[]{:S(2)}, u32[]{:S(2)}) collective-permute-start(f32[1,1,1,224,768]{4,3,2,1,0:T(8,128)S(1)} %slice.151), channel_id=1, source_target_pairs={{0,12},{1,13},{2,14},{3,15},{4,0},{5,1},{6,2},{7,3},{8,4},{9,5},{1... | collective-permute-start | bytes 2064392 | tf_op jit(solution)/shard_map/ppermute | solution.py:147
  107.0 153.9 %collective-permute-start.10 = (f32[4,1,1,448,384]{4,3,2,1,0:T(8,128)}, f32[4,1,1,448,384]{4,3,2,1,0:T(8,128)}, u32[]{:S(2)}, u32[]{:S(2)}) collective-permute-start(f32[4,1,1,448,384]{4,3,2,1,0:T(8,128)} %get-tuple-element.30), channel_id=1, source_target_pairs={{0,1},{1,0},{2,3},{3,2},{4,5},{5,4},{6,7},{7,6},{8,9},{9,8},{10,11... | collective-permute-start | bytes 8257544 | tf_op jit(solution)/shard_map/ppermute | solution.py:147
  108.5 159.2 %collective-permute-start.11 = (f32[4,1,1,448,384]{4,3,2,1,0:T(8,128)}, f32[4,1,1,448,384]{4,3,2,1,0:T(8,128)}, u32[]{:S(2)}, u32[]{:S(2)}) collective-permute-start(f32[4,1,1,448,384]{4,3,2,1,0:T(8,128)} %get-tuple-element.27), channel_id=1, source_target_pairs={{0,2},{1,3},{2,0},{3,1},{4,6},{5,7},{6,4},{7,5},{8,10},{9,11},{10,... | collective-permute-start | bytes 8257544 | tf_op jit(solution)/shard_map/ppermute | solution.py:147
  110.1 63.6 %collective-permute-start.12 = (f32[1,1,1,448,128]{4,3,2,1,0:T(8,128)S(1)}, f32[1,1,1,448,128]{4,3,2,1,0:T(8,128)S(1)}, u32[]{:S(2)}, u32[]{:S(2)}) collective-permute-start(f32[1,1,1,448,128]{4,3,2,1,0:T(8,128)S(1)} %slice_bitcast_fusion.3), channel_id=1, source_target_pairs={{0,1},{1,0},{2,3},{3,2},{4,5},{5,4},{6,7},{7,6},{8,9},{9,8},{10,11... | collective-permute-start | bytes 688136 | tf_op jit(solution)/shard_map/ppermute | solution.py:147
  174.4 11.8 %collective-permute-start.13 = (f32[1,1,2,448,128]{4,3,2,1,0:T(8,128)}, f32[1,1,2,448,128]{4,3,2,1,0:T(8,128)S(1)}, u32[]{:S(2)}, u32[]{:S(2)}) collective-permute-start(f32[1,1,2,448,128]{4,3,2,1,0:T(8,128)} %constant_dynamic-update-slice_fusion.46), channel_id=1, source_target_pairs={{0,2},{1,3},{2,0},{3,1},{4,6},{5,7},{6,4},{7,5},{8,10},{9,11},{10,... | collective-permute-start | bytes 1376264 | tf_op jit(solution)/shard_map/ppermute | solution.py:147
  187.0 65.5 %collective-permute-start.14 = (f32[1,2,2,448,128]{4,3,2,1,0:T(8,128)}, f32[1,2,2,448,128]{4,3,2,1,0:T(8,128)S(1)}, u32[]{:S(2)}, u32[]{:S(2)}) collective-permute-start(f32[1,2,2,448,128]{4,3,2,1,0:T(8,128)} %constant_dynamic-update-slice_fusion.44), channel_id=1, source_target_pairs={{0,4},{1,5},{2,6},{3,7},{4,8},{5,9},{6,10},{7,11},{8,12},{9,13},{1... | collective-permute-start | bytes 2752520 | tf_op jit(solution)/shard_map/ppermute | solution.py:147
  187.6 65.0 %collective-permute-start.15 = (f32[1,2,2,448,128]{4,3,2,1,0:T(8,128)}, f32[1,2,2,448,128]{4,3,2,1,0:T(8,128)}, u32[]{:S(2)}, u32[]{:S(2)}) collective-permute-start(f32[1,2,2,448,128]{4,3,2,1,0:T(8,128)} %constant_dynamic-update-slice_fusion.44), channel_id=1, source_target_pairs={{0,12},{1,13},{2,14},{3,15},{4,0},{5,1},{6,2},{7,3},{8,4},{9,5},{1... | collective-permute-start | bytes 2752520 | tf_op jit(solution)/shard_map/ppermute | solution.py:147
  193.9 34.0 %collective-permute-start.2 = (f32[8,128]{1,0:T(8,128)S(1)}, f32[8,128]{1,0:T(8,128)S(1)}, u32[]{:S(2)}, u32[]{:S(2)}) collective-permute-start(f32[8,128]{1,0:T(8,128)S(1)} %broadcast_in_dim.13), channel_id=1, source_target_pairs={{0,12},{1,13},{2,14},{3,15},{4,0},{5,1},{6,2},{7,3},{8,4},{9,5},{1... | collective-permute-start | bytes 12296 | tf_op jit(solution)/shard_map/ppermute | solution.py:227
  227.9 4.5 collective-permute-start.1
  232.4 5.4 collective-permute-start
  238.4 4.6 collective-permute-start.5
  243.0 3.6 collective-permute-start.4
  246.6 3.6 collective-permute-start.3
  248.1 3.4 copy-start.9
  252.5 22.0 %collective-permute-start.16 = (f32[1,1,2,448,128]{4,3,2,1,0:T(8,128)S(1)}, f32[1,1,2,448,128]{4,3,2,1,0:T(8,128)S(1)}, u32[]{:S(2)}, u32[]{:S(2)}) collective-permute-start(f32[1,1,2,448,128]{4,3,2,1,0:T(8,128)S(1)} %slice.157), channel_id=1, source_target_pairs={{0,4},{1,5},{2,6},{3,7},{4,8},{5,9},{6,10},{7,11},{8,12},{9,13},{1... | collective-permute-start | bytes 1376264 | tf_op jit(solution)/shard_map/ppermute | solution.py:147
  253.6 20.9 %collective-permute-start.17 = (f32[1,1,2,448,128]{4,3,2,1,0:T(8,128)S(1)}, f32[1,1,2,448,128]{4,3,2,1,0:T(8,128)S(1)}, u32[]{:S(2)}, u32[]{:S(2)}) collective-permute-start(f32[1,1,2,448,128]{4,3,2,1,0:T(8,128)S(1)} %slice.158), channel_id=1, source_target_pairs={{0,12},{1,13},{2,14},{3,15},{4,0},{5,1},{6,2},{7,3},{8,4},{9,5},{1... | collective-permute-start | bytes 1376264 | tf_op jit(solution)/shard_map/ppermute | solution.py:147
  258.5 5.9 copy-start.4
  265.9 33.1 %collective-permute-start.18 = (f32[1,1,2,448,384]{4,3,2,1,0:T(8,128)S(1)}, f32[1,1,2,448,384]{4,3,2,1,0:T(8,128)S(1)}, u32[]{:S(2)}, u32[]{:S(2)}) collective-permute-start(f32[1,1,2,448,384]{4,3,2,1,0:T(8,128)S(1)} %get-tuple-element.26), channel_id=1, source_target_pairs={{0,2},{1,3},{2,0},{3,1},{4,6},{5,7},{6,4},{7,5},{8,10},{9,11},{10,... | collective-permute-start | bytes 4128776 | tf_op jit(solution)/shard_map/ppermute | solution.py:147
  267.6 6.9 copy-start.1
  272.9 31.5 %collective-permute-start.19 = (f32[1,2,1,448,384]{4,3,2,1,0:T(8,128)S(1)}, f32[1,2,1,448,384]{4,3,2,1,0:T(8,128)S(1)}, u32[]{:S(2)}, u32[]{:S(2)}) collective-permute-start(f32[1,2,1,448,384]{4,3,2,1,0:T(8,128)S(1)} %get-tuple-element.24), channel_id=1, source_target_pairs={{0,1},{1,0},{2,3},{3,2},{4,5},{5,4},{6,7},{7,6},{8,9},{9,8},{10,11... | collective-permute-start | bytes 4128776 | tf_op jit(solution)/shard_map/ppermute | solution.py:147
  279.1 99.9 %collective-permute-start.22 = (f32[3,1,2,448,384]{4,3,2,1,0:T(8,128)}, f32[3,1,2,448,384]{4,3,2,1,0:T(8,128)}, u32[]{:S(2)}, u32[]{:S(2)}) collective-permute-start(f32[3,1,2,448,384]{4,3,2,1,0:T(8,128)} %slice.162), channel_id=1, source_target_pairs={{0,2},{1,3},{2,0},{3,1},{4,6},{5,7},{6,4},{7,5},{8,10},{9,11},{10,... | collective-permute-start | bytes 12386312 | tf_op jit(solution)/shard_map/ppermute | solution.py:147
  294.7 90.9 %collective-permute-start.23 = (f32[3,2,1,448,384]{4,3,2,1,0:T(8,128)}, f32[3,2,1,448,384]{4,3,2,1,0:T(8,128)}, u32[]{:S(2)}, u32[]{:S(2)}) collective-permute-start(f32[3,2,1,448,384]{4,3,2,1,0:T(8,128)} %slice.163), channel_id=1, source_target_pairs={{0,1},{1,0},{2,3},{3,2},{4,5},{5,4},{6,7},{7,6},{8,9},{9,8},{10,11... | collective-permute-start | bytes 12386312 | tf_op jit(solution)/shard_map/ppermute | solution.py:147
  307.5 82.6 %collective-permute-start.20 = (f32[896,896]{1,0:T(8,128)}, f32[896,896]{1,0:T(8,128)}, u32[]{:S(2)}, u32[]{:S(2)}) collective-permute-start(f32[896,896]{1,0:T(8,128)} %bitcast.7), channel_id=1, source_target_pairs={{0,16},{16,0},{1,17},{17,1},{2,18},{18,2},{3,19},{19,3},{4,20},{20... | collective-permute-start | bytes 9633800 | tf_op jit(solution)/shard_map/ppermute | solution.py:236
  307.7 160.6 %collective-permute-start.21 = (f32[448,896]{1,0:T(8,128)S(1)}, f32[448,896]{1,0:T(8,128)S(1)}, u32[]{:S(2)}, u32[]{:S(2)}) collective-permute-start(f32[448,896]{1,0:T(8,128)S(1)} %broadcast_multiply_fusion), channel_id=1, source_target_pairs={{0,16},{16,0},{1,17},{17,1},{2,18},{18,2},{3,19},{19,3},{4,20},{20... | collective-permute-start | bytes 4816904 | tf_op jit(solution)/shard_map/ppermute | solution.py:236
  468.3 8.0 copy-start
  482.3 27.5 %copy-start.5 = (bf16[1,448,2048]{2,1,0:T(8,128)(2,1)S(1)}, bf16[1,448,2048]{2,1,0:T(8,128)(2,1)}, u32[]{:S(2)}) copy-start(bf16[1,448,2048]{2,1,0:T(8,128)(2,1)} %param.3) | copy-start | bytes 5505028
  509.8 403.2 %collective-permute-start.24 = (f32[448,7168]{1,0:T(8,128)}, f32[448,7168]{1,0:T(8,128)}, u32[]{:S(2)}, u32[]{:S(2)}) collective-permute-start(f32[448,7168]{1,0:T(8,128)} %fusion.2), channel_id=1, source_target_pairs={{0,16},{16,0},{1,17},{17,1},{2,18},{18,2},{3,19},{19,3},{4,20},{20... | collective-permute-start | bytes 38535176 | tf_op jit(solution)/shard_map/ppermute | solution.py:236
  509.8 13.0 %collective-permute-start.25 = (bf16[1,1,1,448,512]{4,3,2,1,0:T(8,128)(2,1)S(1)}, bf16[1,1,1,448,512]{4,3,2,1,0:T(8,128)(2,1)S(1)}, u32[]{:S(2)}, u32[]{:S(2)}) collective-permute-start(bf16[1,1,1,448,512]{4,3,2,1,0:T(8,128)(2,1)S(1)} %slice_bitcast_fusion.2), channel_id=1, source_target_pairs={{0,1},{1,0},{2,3},{3,2},{4,5},{5,4},{6,7},{7,6},{8,9},{9,8},{10,11... | collective-permute-start | bytes 1376264 | tf_op jit(solution)/shard_map/ppermute | solution.py:147
  523.6 22.2 %collective-permute-start.26 = (bf16[1,1,2,448,512]{4,3,2,1,0:T(8,128)(2,1)}, bf16[1,1,2,448,512]{4,3,2,1,0:T(8,128)(2,1)}, u32[]{:S(2)}, u32[]{:S(2)}) collective-permute-start(bf16[1,1,2,448,512]{4,3,2,1,0:T(8,128)(2,1)} %constant_dynamic-update-slice_fusion.28), channel_id=1, source_target_pairs={{0,2},{1,3},{2,0},{3,1},{4,6},{5,7},{6,4},{7,5},{8,10},{9,11},{10,... | collective-permute-start | bytes 2752520 | tf_op jit(solution)/shard_map/ppermute | solution.py:147
  527.3 35.3 %collective-permute-start.27 = (bf16[1,1,1,448,1536]{4,3,2,1,0:T(8,128)(2,1)}, bf16[1,1,1,448,1536]{4,3,2,1,0:T(8,128)(2,1)S(1)}, u32[]{:S(2)}, u32[]{:S(2)}) collective-permute-start(bf16[1,1,1,448,1536]{4,3,2,1,0:T(8,128)(2,1)} %slice_bitcast_fusion.1), channel_id=1, source_target_pairs={{0,4},{1,5},{2,6},{3,7},{4,8},{5,9},{6,10},{7,11},{8,12},{9,13},{1... | collective-permute-start | bytes 4128776 | tf_op jit(solution)/shard_map/ppermute | solution.py:147
  548.0 53.8 %collective-permute-start.33 = (bf16[1,2,2,448,512]{4,3,2,1,0:T(8,128)(2,1)}, bf16[1,2,2,448,512]{4,3,2,1,0:T(8,128)(2,1)}, u32[]{:S(2)}, u32[]{:S(2)}) collective-permute-start(bf16[1,2,2,448,512]{4,3,2,1,0:T(8,128)(2,1)} %constant_dynamic-update-slice_fusion.26), channel_id=1, source_target_pairs={{0,4},{1,5},{2,6},{3,7},{4,8},{5,9},{6,10},{7,11},{8,12},{9,13},{1... | collective-permute-start | bytes 5505032 | tf_op jit(solution)/shard_map/ppermute | solution.py:147
  548.0 81.8 %collective-permute-start.28 = (bf16[1,1,1,448,1536]{4,3,2,1,0:T(8,128)(2,1)}, bf16[1,1,1,448,1536]{4,3,2,1,0:T(8,128)(2,1)}, u32[]{:S(2)}, u32[]{:S(2)}) collective-permute-start(bf16[1,1,1,448,1536]{4,3,2,1,0:T(8,128)(2,1)} %slice_bitcast_fusion.1), channel_id=1, source_target_pairs={{0,12},{1,13},{2,14},{3,15},{4,0},{5,1},{6,2},{7,3},{8,4},{9,5},{1... | collective-permute-start | bytes 4128776 | tf_op jit(solution)/shard_map/ppermute | solution.py:147
  551.9 175.8 %collective-permute-start.34 = (bf16[1,2,2,448,512]{4,3,2,1,0:T(8,128)(2,1)}, bf16[1,2,2,448,512]{4,3,2,1,0:T(8,128)(2,1)S(1)}, u32[]{:S(2)}, u32[]{:S(2)}) collective-permute-start(bf16[1,2,2,448,512]{4,3,2,1,0:T(8,128)(2,1)} %constant_dynamic-update-slice_fusion.26), channel_id=1, source_target_pairs={{0,12},{1,13},{2,14},{3,15},{4,0},{5,1},{6,2},{7,3},{8,4},{9,5},{1... | collective-permute-start | bytes 5505032 | tf_op jit(solution)/shard_map/ppermute | solution.py:147
  562.6 122.8 %collective-permute-start.29 = (bf16[1,1,1,224,1536]{4,3,2,1,0:T(8,128)(2,1)S(1)}, bf16[1,1,1,224,1536]{4,3,2,1,0:T(8,128)(2,1)S(1)}, u32[]{:S(2)}, u32[]{:S(2)}) collective-permute-start(bf16[1,1,1,224,1536]{4,3,2,1,0:T(8,128)(2,1)S(1)} %slice.165), channel_id=1, source_target_pairs={{0,4},{1,5},{2,6},{3,7},{4,8},{5,9},{6,10},{7,11},{8,12},{9,13},{1... | collective-permute-start | bytes 2064392 | tf_op jit(solution)/shard_map/ppermute | solution.py:147
  603.1 124.9 %collective-permute-start.35 = (bf16[1,1,2,448,512]{4,3,2,1,0:T(8,128)(2,1)S(1)}, bf16[1,1,2,448,512]{4,3,2,1,0:T(8,128)(2,1)S(1)}, u32[]{:S(2)}, u32[]{:S(2)}) collective-permute-start(bf16[1,1,2,448,512]{4,3,2,1,0:T(8,128)(2,1)S(1)} %slice.169), channel_id=1, source_target_pairs={{0,4},{1,5},{2,6},{3,7},{4,8},{5,9},{6,10},{7,11},{8,12},{9,13},{1... | collective-permute-start | bytes 2752520 | tf_op jit(solution)/shard_map/ppermute | solution.py:147
  631.0 87.1 %collective-permute-start.30 = (bf16[1,1,1,224,1536]{4,3,2,1,0:T(8,128)(2,1)S(1)}, bf16[1,1,1,224,1536]{4,3,2,1,0:T(8,128)(2,1)S(1)}, u32[]{:S(2)}, u32[]{:S(2)}) collective-permute-start(bf16[1,1,1,224,1536]{4,3,2,1,0:T(8,128)(2,1)S(1)} %slice.166), channel_id=1, source_target_pairs={{0,12},{1,13},{2,14},{3,15},{4,0},{5,1},{6,2},{7,3},{8,4},{9,5},{1... | collective-permute-start | bytes 2064392 | tf_op jit(solution)/shard_map/ppermute | solution.py:147
  724.2 33.1 %collective-permute-start.31 = (bf16[4,1,1,448,384]{4,3,2,1,0:T(8,128)(2,1)S(1)}, bf16[4,1,1,448,384]{4,3,2,1,0:T(8,128)(2,1)S(1)}, u32[]{:S(2)}, u32[]{:S(2)}) collective-permute-start(bf16[4,1,1,448,384]{4,3,2,1,0:T(8,128)(2,1)S(1)} %get-tuple-element.22), channel_id=1, source_target_pairs={{0,1},{1,0},{2,3},{3,2},{4,5},{5,4},{6,7},{7,6},{8,9},{9,8},{10,11... | collective-permute-start | bytes 4128776 | tf_op jit(solution)/shard_map/ppermute | solution.py:147
  725.8 33.1 %collective-permute-start.32 = (bf16[4,1,1,448,384]{4,3,2,1,0:T(8,128)(2,1)S(1)}, bf16[4,1,1,448,384]{4,3,2,1,0:T(8,128)(2,1)S(1)}, u32[]{:S(2)}, u32[]{:S(2)}) collective-permute-start(bf16[4,1,1,448,384]{4,3,2,1,0:T(8,128)(2,1)S(1)} %get-tuple-element.21), channel_id=1, source_target_pairs={{0,2},{1,3},{2,0},{3,1},{4,6},{5,7},{6,4},{7,5},{8,10},{9,11},{10,... | collective-permute-start | bytes 4128776 | tf_op jit(solution)/shard_map/ppermute | solution.py:147
  727.6 34.3 %copy-start.7 = (bf16[1,2,2,448,512]{4,3,2,1,0:T(8,128)(2,1)}, bf16[1,2,2,448,512]{4,3,2,1,0:T(8,128)(2,1)S(1)}, u32[]{:S(2)}) copy-start(bf16[1,2,2,448,512]{4,3,2,1,0:T(8,128)(2,1)S(1)} %collective-permute-done.34) | copy-start | bytes 5505028
  727.6 58.2 %collective-permute-start.40 = (bf16[4,1,1,448,384]{4,3,2,1,0:T(8,128)(2,1)S(1)}, bf16[4,1,1,448,384]{4,3,2,1,0:T(8,128)(2,1)S(1)}, u32[]{:S(2)}, u32[]{:S(2)}) collective-permute-start(bf16[4,1,1,448,384]{4,3,2,1,0:T(8,128)(2,1)S(1)} %get-tuple-element.20), channel_id=1, source_target_pairs={{0,1},{1,0},{2,3},{3,2},{4,5},{5,4},{6,7},{7,6},{8,9},{9,8},{10,11... | collective-permute-start | bytes 4128776 | tf_op jit(solution)/shard_map/ppermute | solution.py:147
  728.1 33.9 %copy-start.10 = (bf16[1,1,2,448,512]{4,3,2,1,0:T(8,128)(2,1)}, bf16[1,1,2,448,512]{4,3,2,1,0:T(8,128)(2,1)S(1)}, u32[]{:S(2)}) copy-start(bf16[1,1,2,448,512]{4,3,2,1,0:T(8,128)(2,1)S(1)} %collective-permute-done.35) | copy-start | bytes 2752516
  728.1 60.6 %collective-permute-start.41 = (bf16[4,1,1,448,384]{4,3,2,1,0:T(8,128)(2,1)S(1)}, bf16[4,1,1,448,384]{4,3,2,1,0:T(8,128)(2,1)S(1)}, u32[]{:S(2)}, u32[]{:S(2)}) collective-permute-start(bf16[4,1,1,448,384]{4,3,2,1,0:T(8,128)(2,1)S(1)} %get-tuple-element.15), channel_id=1, source_target_pairs={{0,2},{1,3},{2,0},{3,1},{4,6},{5,7},{6,4},{7,5},{8,10},{9,11},{10,... | collective-permute-start | bytes 4128776 | tf_op jit(solution)/shard_map/ppermute | solution.py:147
  757.3 34.4 %collective-permute-start.36 = (bf16[1,1,2,448,512]{4,3,2,1,0:T(8,128)(2,1)S(1)}, bf16[1,1,2,448,512]{4,3,2,1,0:T(8,128)(2,1)S(1)}, u32[]{:S(2)}, u32[]{:S(2)}) collective-permute-start(bf16[1,1,2,448,512]{4,3,2,1,0:T(8,128)(2,1)S(1)} %slice.170), channel_id=1, source_target_pairs={{0,12},{1,13},{2,14},{3,15},{4,0},{5,1},{6,2},{7,3},{8,4},{9,5},{1... | collective-permute-start | bytes 2752520 | tf_op jit(solution)/shard_map/ppermute | solution.py:147
  758.9 88.6 %collective-permute-start.37 = (bf16[4,1,2,448,384]{4,3,2,1,0:T(8,128)(2,1)}, bf16[4,1,2,448,384]{4,3,2,1,0:T(8,128)(2,1)}, u32[]{:S(2)}, u32[]{:S(2)}) collective-permute-start(bf16[4,1,2,448,384]{4,3,2,1,0:T(8,128)(2,1)} %constant_dynamic-update-slice_fusion.18), channel_id=1, source_target_pairs={{0,2},{1,3},{2,0},{3,1},{4,6},{5,7},{6,4},{7,5},{8,10},{9,11},{10,... | collective-permute-start | bytes 8257544 | tf_op jit(solution)/shard_map/ppermute | solution.py:147
  785.8 65.3 %collective-permute-start.38 = (bf16[4,2,1,448,384]{4,3,2,1,0:T(8,128)(2,1)}, bf16[4,2,1,448,384]{4,3,2,1,0:T(8,128)(2,1)}, u32[]{:S(2)}, u32[]{:S(2)}) collective-permute-start(bf16[4,2,1,448,384]{4,3,2,1,0:T(8,128)(2,1)} %constant_dynamic-update-slice_fusion.15), channel_id=1, source_target_pairs={{0,1},{1,0},{2,3},{3,2},{4,5},{5,4},{6,7},{7,6},{8,9},{9,8},{10,11... | collective-permute-start | bytes 8257544 | tf_op jit(solution)/shard_map/ppermute | solution.py:147
  788.7 116.6 %collective-permute-start.42 = (bf16[4,1,2,448,384]{4,3,2,1,0:T(8,128)(2,1)}, bf16[4,1,2,448,384]{4,3,2,1,0:T(8,128)(2,1)}, u32[]{:S(2)}, u32[]{:S(2)}) collective-permute-start(bf16[4,1,2,448,384]{4,3,2,1,0:T(8,128)(2,1)} %constant_dynamic-update-slice_fusion.6), channel_id=1, source_target_pairs={{0,2},{1,3},{2,0},{3,1},{4,6},{5,7},{6,4},{7,5},{8,10},{9,11},{10,... | collective-permute-start | bytes 8257544 | tf_op jit(solution)/shard_map/ppermute | solution.py:147
  792.6 116.4 %collective-permute-start.43 = (bf16[4,2,1,448,384]{4,3,2,1,0:T(8,128)(2,1)}, bf16[4,2,1,448,384]{4,3,2,1,0:T(8,128)(2,1)}, u32[]{:S(2)}, u32[]{:S(2)}) collective-permute-start(bf16[4,2,1,448,384]{4,3,2,1,0:T(8,128)(2,1)} %constant_dynamic-update-slice_fusion.3), channel_id=1, source_target_pairs={{0,1},{1,0},{2,3},{3,2},{4,5},{5,4},{6,7},{7,6},{8,9},{9,8},{10,11... | collective-permute-start | bytes 8257544 | tf_op jit(solution)/shard_map/ppermute | solution.py:147
  793.1 1.5 copy-start.6
  799.7 6.9 copy-start.8
  803.6 4.5 copy-start.11
  806.5 2.5 copy-start.13
  909.0 24.2 %slice-start = ((s8[18350080]{0:T(1024)(128)(4,1)}), s8[4194304]{0:T(1024)(128)(4,1)S(1)}, s32[]{:S(2)}) async-start(s8[18350080]{0:T(1024)(128)(4,1)} %bitcast.38), calls=%async_computation | async-start | bytes 8388608
  912.9 20.3 %slice-start.1 = ((s8[18350080]{0:T(1024)(128)(4,1)}), s8[4194304]{0:T(1024)(128)(4,1)S(1)}, s32[]{:S(2)}) async-start(s8[18350080]{0:T(1024)(128)(4,1)} %bitcast.38), calls=%async_computation.1 | async-start | bytes 8388608
  912.9 20.3 %slice-start.2 = ((s8[18350080]{0:T(1024)(128)(4,1)}), s8[4194304]{0:T(1024)(128)(4,1)S(1)}, s32[]{:S(2)}) async-start(s8[18350080]{0:T(1024)(128)(4,1)} %bitcast.38), calls=%async_computation.2 | async-start | bytes 8388608
  912.9 20.3 %slice-start.3 = ((s8[18350080]{0:T(1024)(128)(4,1)}), s8[4194304]{0:T(1024)(128)(4,1)S(1)}, s32[]{:S(2)}) async-start(s8[18350080]{0:T(1024)(128)(4,1)} %bitcast.38), calls=%async_computation.3 | async-start | bytes 8388608
  913.0 20.3 %slice-start.4 = ((s8[18350080]{0:T(1024)(128)(4,1)}), s8[1572864]{0:T(1024)(128)(4,1)S(1)}, s32[]{:S(2)}) async-start(s8[18350080]{0:T(1024)(128)(4,1)} %bitcast.38), calls=%async_computation.4 | async-start | bytes 3145728
  954.9 2.1 copy-start.2
  958.7 21.1 %collective-permute-start.39 = (f32[448,1280]{1,0:T(8,128)}, f32[448,1280]{1,0:T(8,128)S(1)}, u32[]{:S(2)}, u32[]{:S(2)}) collective-permute-start(f32[448,1280]{1,0:T(8,128)} %slice_add_fusion), channel_id=1, source_target_pairs={{0,16},{16,0},{1,17},{17,1},{2,18},{18,2},{3,19},{19,3},{4,20},{20... | collective-permute-start | bytes 6881288 | tf_op jit(solution)/shard_map/ppermute | solution.py:236
  976.2 3.6 copy-start.3
  976.2 3.3 collective-permute-start.44
  980.9 1.8 copy-start.14
  (1 other events, 0.9 us)
